TPU v7x, 32 devices: a whole 2x2x4 slice. The times are simulated.
32 devices in a mesh: chain: 8 (over y, x, core), col: 4 (over z).
Axes of the slice: x: 2, y: 2, z: 4, core: 2. Of those that a mesh axis runs over, the one named last changes fastest.
Arguments:
- rhs: bfloat16 [16, 64, 2560], P('chain', None, 'col'), may hold values from -6 to 6
- block_inverse: bfloat16 [16, 2560, 2560], P('chain', 'col'), as said below
- entry_factor: bfloat16 [16, 2560, 128], P('chain', 'col'), as said below
- exit_factor: bfloat16 [16, 2560, 128], P('chain', 'col'), as said below
- previous: bfloat16 [64, 2560], P(None, 'col'), may hold values from -6 to 6
Outputs:
- solution: float32 [16, 64, 2560], P('chain', None, 'col')
Inputs may be any that keep to these rules, and one draw needn't show every extreme that they name: Every block of block_inverse equals its own transpose. `entry_factor`: entries are independent, of mean zero. `exit_factor`: entries are independent, of mean zero.
All inputs are finite; a program needn't handle non-finite values.
Results may differ from a plain program's by a relative error of at most 0.0003.
Values may be sent and summed in bfloat16 or wider, within the bound.
A program may use at most 64 MiB of HBM per device.

v0:
```python
import functools

import jax
import jax.numpy as jnp
from jax import lax
from jax.experimental import pallas as pl
from jax.experimental.pallas import tpu as pltpu
from jax.sharding import PartitionSpec as P

MESH = pl.DeviceIdType.MESH
F32 = jnp.float32
BF16 = jnp.bfloat16


def dot_t(a, b):
    return lax.dot_general(a, b, (((1,), (1,)), ((), ())), preferred_element_type=F32)


def terms(x):
    first = x.astype(BF16)
    rest = x - first.astype(F32)
    second = rest.astype(BF16)
    third = (rest - second.astype(F32)).astype(BF16)
    return first, second, third


def split_dot_t(x, low):
    rows = x.shape[0]
    product = dot_t(jnp.concatenate(terms(x), axis=0), low)
    return (product[2 * rows:] + product[rows:2 * rows]) + product[:rows]


def exact_dot(a, b):
    a1, a2, a3 = terms(a)
    b1, b2, b3 = terms(b)
    return jnp.dot(
        jnp.concatenate([a3, a2, a1, a2, a1, a1], axis=1),
        jnp.concatenate([b1, b2, b3, b1, b2, b1], axis=0),
        preferred_element_type=F32,
    )


def exact_dot_t(a, b):
    a1, a2, a3 = terms(a)
    b1, b2, b3 = terms(b)
    return dot_t(
        jnp.concatenate([a3, a2, a1, a2, a1, a1], axis=1),
        jnp.concatenate([b1, b2, b3, b1, b2, b1], axis=1),
    )


def kernel(
    n, m, rhs_hbm, binv_hbm, entry_hbm, exit_hbm, prev_hbm, out_ref,
    rhs, binv, entry, exits, prev, arriving,
    parts, parts_in, opening, opening_in, summed, comp, gathered,
    states, forward, applied, carried, carried_in, carried_sum, back, back_in, behind,
    local_sem, exit_sem, part_send, part_recv, open_send, open_recv,
    comp_send, comp_recv, state_send, state_recv, fwd_send, fwd_recv,
    car_send, car_recv, back_send, back_recv, beh_send, beh_recv,
):
    c = lax.axis_index("chain")
    k = lax.axis_index("col")
    count, columns, width = rhs.shape
    nx = entry.shape[2]

    def owner_of(chain):
        return m // 2 - 1 + lax.rem(chain, 2)

    owner = owner_of(c)
    is_owner = k == owner
    unsent = []

    def remote(src, dst, send, recv, where):
        return pltpu.make_async_remote_copy(
            src_ref=src, dst_ref=dst, send_sem=send, recv_sem=recv,
            device_id=where, device_id_type=MESH,
        )

    def send(condition, *args):
        @pl.when(condition)
        def _():
            remote(*args).start()

        unsent.append((condition, args))

    loads = [
        pltpu.make_async_copy(exit_hbm, exits, local_sem.at[0]),
        pltpu.make_async_copy(entry_hbm, entry, local_sem.at[1]),
        pltpu.make_async_copy(rhs_hbm, rhs, local_sem.at[2]),
        pltpu.make_async_copy(prev_hbm, prev, local_sem.at[3]),
    ] + [
        pltpu.make_async_copy(binv_hbm.at[p], binv.at[p], local_sem.at[4 + p])
        for p in range(count)
    ]
    for load in loads:
        load.start()

    barrier = pltpu.get_barrier_semaphore()
    for d in range(1, m):
        pl.semaphore_signal(
            barrier, 1, device_id={"col": lax.rem(k + d, m)}, device_id_type=MESH
        )

    @pl.when(c > 0)
    def _():
        pl.semaphore_signal(barrier, 1, device_id={"chain": c - 1}, device_id_type=MESH)

    @pl.when(c < n - 1)
    def _():
        pl.semaphore_signal(barrier, 1, device_id={"chain": c + 1}, device_id_type=MESH)

    @pl.when(is_owner)
    def _():
        for d in range(1, n):
            other = lax.rem(c + d, n)
            pl.semaphore_signal(
                barrier, 1, device_id={"chain": other, "col": owner_of(other)},
                device_id_type=MESH,
            )

    @pl.when(c == n - 1)
    def _():
        arriving[...] = jnp.zeros_like(arriving)

    for load in loads[:4]:
        load.wait()

    @pl.when(c == 0)
    def _():
        opening[...] = jnp.dot(prev[...], exits[0], preferred_element_type=F32)

    def following(p):
        return exits[p + 1] if p + 1 < count else arriving[...]

    def part(p):
        parts[p, :nx] = -lax.dot_general(
            entry[p], following(p), (((0,), (0,)), ((), ())), preferred_element_type=F32
        )
        parts[p, nx:] = jnp.dot(rhs[p], following(p), preferred_element_type=F32)

    for p in range(count - 1):
        part(p)

    expected = m - 1 + jnp.where(c > 0, 1, 0) + jnp.where(c < n - 1, 1, 0)
    pl.semaphore_wait(barrier, expected + jnp.where(is_owner, n - 1, 0))

    send(c > 0, exits.at[0], arriving, exit_sem.at[0], exit_sem.at[1], {"chain": c - 1})
    send(
        (c == 0) & jnp.logical_not(is_owner), opening, opening_in.at[k],
        open_send, open_recv.at[k], {"col": owner},
    )

    for p in range(count):
        if p + 1 == count:
            @pl.when(c < n - 1)
            def _():
                remote(
                    exits.at[0], arriving, exit_sem.at[0], exit_sem.at[1], {"chain": c}
                ).wait_recv()
            part(p)
        send(
            jnp.logical_not(is_owner), parts.at[p], parts_in.at[k, p],
            part_send.at[p], part_recv.at[k, p], {"col": owner},
        )

    def spread(buffer, p, sends, recvs):
        for d in range(1, m):
            send(
                is_owner, buffer.at[p], buffer.at[p], sends.at[p, d - 1], recvs.at[p],
                {"col": lax.rem(k + d, m)},
            )

    @pl.when(is_owner)
    def _():
        for p in range(count):
            for d in range(1, m):
                other = lax.rem(k + d, m)
                remote(
                    parts.at[p], parts_in.at[other, p], part_send.at[p],
                    part_recv.at[other, p], {"col": other},
                ).wait_recv()
            total = parts[p]
            for d in range(1, m):
                total += parts_in[lax.rem(k + d, m), p]
            summed[p] = total
        both = summed[0]
        for p in range(1, count):
            both = exact_dot(both, summed[p, :nx])
            both = jnp.concatenate([both[:nx], both[nx:] + summed[p, nx:]], axis=0)
        comp[...] = both

        @pl.when(c == 0)
        def _():
            total = opening[...]
            for d in range(1, m):
                other = lax.rem(k + d, m)
                remote(
                    opening, opening_in.at[other], open_send,
                    open_recv.at[other], {"col": other},
                ).wait_recv()
                total += opening_in[other]
            states[0] = total
            comp[nx:] = exact_dot(total, comp[:nx]) + comp[nx:]

    for d in range(1, n):
        later = lax.rem(c + d, n)
        there = {"chain": later, "col": owner_of(later)}
        send(
            is_owner & (c > 0) & (c + d < n), comp, gathered.at[c], comp_send.at[d - 1],
            comp_recv.at[c], there,
        )
        send(
            is_owner & (c == 0), comp.at[pl.ds(nx, columns)],
            gathered.at[c, pl.ds(nx, columns)], comp_send.at[d - 1], comp_recv.at[c], there,
        )
    for d in range(1, n):
        earlier = lax.rem(c - d + n, n)
        send(
            is_owner & (c - d >= 0), comp.at[pl.ds(0, nx)], gathered.at[c, pl.ds(0, nx)],
            comp_send.at[n - 1 + d - 1], comp_recv.at[c],
            {"chain": earlier, "col": owner_of(earlier)},
        )

    @pl.when(is_owner & (c > 0))
    def _():
        def fold(s, state):
            remote(
                comp, gathered.at[s], comp_send.at[0], comp_recv.at[s], {"chain": c}
            ).wait_recv()
            return exact_dot(state, gathered[s, :nx]) + gathered[s, nx:]

        remote(
            comp.at[pl.ds(nx, columns)], gathered.at[0, pl.ds(nx, columns)],
            comp_send.at[0], comp_recv.at[0], {"chain": c},
        ).wait_recv()
        states[0] = lax.fori_loop(1, c, fold, gathered[0, nx:])

    for p in range(count):
        if p > 0:
            @pl.when(is_owner)
            def _():
                states[p] = exact_dot(states[p - 1], summed[p - 1, :nx]) + summed[p - 1, nx:]
        spread(states, p, state_send, state_recv)

    for p in range(count):
        @pl.when(jnp.logical_not(is_owner))
        def _():
            remote(
                states.at[p], states.at[p], state_send.at[p, 0], state_recv.at[p], {"col": k}
            ).wait_recv()
        forward[k, p] = (
            rhs[p].astype(F32) - split_dot_t(states[p], entry[p])
        ).astype(BF16)
        for way, step in ((0, 1), (1, -1)):
            beyond = k + step
            send(
                (beyond >= 0) & (beyond < m), forward.at[k, p], forward.at[k, p],
                fwd_send.at[k, p, way], fwd_recv.at[k, p], {"col": beyond},
            )

    def block(j, p):
        return binv[p, :, pl.ds(pl.multiple_of(j * width, 128), width)]

    for p in range(count):
        loads[4 + p].wait()
        applied[p] = dot_t(forward[k, p], block(k, p))
    for d in range(1, m):
        for p in range(count):
            for way, step in ((0, 1), (1, -1)):
                j = k - step * d
                beyond = k + step
                there = (j >= 0) & (j < m)

                @pl.when(there)
                def _():
                    remote(
                        forward.at[j, p], forward.at[j, p], fwd_send.at[j, p, way],
                        fwd_recv.at[j, p], {"col": j},
                    ).wait_recv()

                send(
                    there & (beyond >= 0) & (beyond < m),
                    forward.at[j, p], forward.at[j, p],
                    fwd_send.at[j, p, way], fwd_recv.at[j, p], {"col": beyond},
                )
            for step in (1, -1):
                j = k - step * d

                @pl.when((j >= 0) & (j < m))
                def _():
                    applied[p] += dot_t(forward[j, p], block(j, p))
            if d == m - 1:
                carried[p] = jnp.dot(
                    applied[p].astype(BF16), entry[p], preferred_element_type=F32
                )
                send(
                    jnp.logical_not(is_owner), carried.at[p], carried_in.at[k, p],
                    car_send.at[p], car_recv.at[k, p], {"col": owner},
                )

    @pl.when(is_owner)
    def _():
        offset = None
        for p in reversed(range(count)):
            total = carried[p]
            for d in range(1, m):
                other = lax.rem(k + d, m)
                remote(
                    carried.at[p], carried_in.at[other, p], car_send.at[p],
                    car_recv.at[other, p], {"col": other},
                ).wait_recv()
                total += carried_in[other, p]
            carried_sum[p] = total
            if offset is None:
                offset = total
            else:
                offset = exact_dot_t(offset, summed[p, :nx]) + total
        back[...] = offset

    for d in range(1, n):
        earlier = lax.rem(c - d + n, n)
        send(
            is_owner & (c - d >= 0), back, back_in.at[c], back_send.at[d - 1],
            back_recv.at[c], {"chain": earlier, "col": owner_of(earlier)},
        )

    @pl.when(is_owner)
    def _():
        def fold(i, state):
            s = n - 1 - i
            remote(
                comp.at[pl.ds(0, nx)], gathered.at[s, pl.ds(0, nx)], comp_send.at[0],
                comp_recv.at[s], {"chain": c},
            ).wait_recv()
            remote(
                back, back_in.at[s], back_send.at[0], back_recv.at[s], {"chain": c}
            ).wait_recv()
            return exact_dot_t(state, gathered[s, :nx]) + back_in[s]

        behind[count - 1] = lax.fori_loop(0, n - 1 - c, fold, jnp.zeros((columns, nx), F32))

    for p in reversed(range(count)):
        if p + 1 < count:
            @pl.when(is_owner)
            def _():
                behind[p] = exact_dot_t(behind[p + 1], summed[p + 1, :nx]) + carried_sum[p + 1]
        spread(behind, p, beh_send, beh_recv)

    for p in reversed(range(count)):
        @pl.when(jnp.logical_not(is_owner))
        def _():
            remote(
                behind.at[p], behind.at[p], beh_send.at[p, 0], beh_recv.at[p], {"col": k}
            ).wait_recv()
        out_ref[p] = applied[p] - split_dot_t(behind[p], following(p))

    for condition, args in unsent:
        @pl.when(condition)
        def _():
            remote(*args).wait_send()


def shards(n, m, rhs, block_inverse, entry_factor, exit_factor, previous):
    count, columns, width = rhs.shape
    nx = entry_factor.shape[2]
    padded = -(-width // 128) * 128
    if padded != width:
        extra = padded - width
        rhs = jnp.pad(rhs, ((0, 0), (0, 0), (0, extra)))
        previous = jnp.pad(previous, ((0, 0), (0, extra)))
        entry_factor = jnp.pad(entry_factor, ((0, 0), (0, extra), (0, 0)))
        exit_factor = jnp.pad(exit_factor, ((0, 0), (0, extra), (0, 0)))
        block_inverse = jnp.pad(
            block_inverse.reshape(count, width, m, width),
            ((0, 0), (0, extra), (0, 0), (0, extra)),
        ).reshape(count, padded, m * padded)
    vmem = pltpu.VMEM
    dma = pltpu.SemaphoreType.DMA
    out = pl.pallas_call(
        functools.partial(kernel, n, m),
        out_shape=jax.ShapeDtypeStruct((count, columns, padded), F32),
        in_specs=[pl.BlockSpec(memory_space=pl.ANY)] * 5,
        out_specs=pl.BlockSpec(memory_space=pltpu.VMEM),
        scratch_shapes=[
            vmem((count, columns, padded), BF16),
            vmem(block_inverse.shape, BF16),
            vmem(entry_factor.shape, BF16),
            vmem(exit_factor.shape, BF16),
            vmem(previous.shape, BF16),
            vmem(exit_factor.shape[1:], BF16),
            vmem((count, nx + columns, nx), F32),
            vmem((m, count, nx + columns, nx), F32),
            vmem((columns, nx), F32),
            vmem((m, columns, nx), F32),
            vmem((count, nx + columns, nx), F32),
            vmem((nx + columns, nx), F32),
            vmem((n, nx + columns, nx), F32),
            vmem((count, columns, nx), F32),
            vmem((m, count, columns, padded), BF16),
            vmem((count, columns, padded), F32),
            vmem((count, columns, nx), F32),
            vmem((m, count, columns, nx), F32),
            vmem((count, columns, nx), F32),
            vmem((columns, nx), F32),
            vmem((n, columns, nx), F32),
            vmem((count, columns, nx), F32),
            dma((4 + count,)),
            dma((2,)),
            dma((count,)), dma((m, count)),
            dma(()), dma((m,)),
            dma((2 * (n - 1),)), dma((n,)),
            dma((count, m - 1)), dma((count,)),
            dma((m, count, 2)), dma((m, count)),
            dma((count,)), dma((m, count)),
            dma((n - 1,)), dma((n,)),
            dma((count, m - 1)), dma((count,)),
        ],
        compiler_params=pltpu.CompilerParams(
            collective_id=0, has_side_effects=True
        ),
    )(rhs, block_inverse, entry_factor, exit_factor, previous)
    return out[:, :, :width] if padded != width else out


def solution(mesh):
    placed = (
        P("chain", None, "col"),
        P("chain", "col", None),
        P("chain", "col", None),
        P("chain", "col", None),
        P(None, "col"),
    )
    return jax.shard_map(
        functools.partial(shards, mesh.shape["chain"], mesh.shape["col"]),
        mesh=mesh, in_specs=placed, out_specs=P("chain", None, "col"), check_vma=False,
    )
```

profile of v0, /device:TPU:0, one launch (start us, length us, event | category | flops | bytes accessed | tf_op | source)
XLA Modules:
  0.0 52.5 jit_solution(15911800497280176965)
XLA Ops:
  0.0 50.8 %shard_map.55 = f32[2,64,640]{2,1,0:T(8,128)} custom-call(bf16[2,64,640]{2,1,0:T(8,128)(2,1)} %rhs_hbm.1, bf16[2,640,2560]{2,1,0:T(8,128)(2,1)} %binv_hbm.1, bf16[2,640,128]{2,1,0:T(8,128)(2,1)} %entry_hbm.1, bf16[2,640,128]{2,1,0:T(8,128)(2,1)} %exit_hbm.1, bf16[64,640]{1,0:T(8,128)(2,1)} %prev_hbm.1), custom_call_target="tpu_custom_call" | custom-call | tf_op jit(solution)/shard_map/pallas_call | solution.py:379
  50.8 1.7 %copy.7 = f32[2,64,640]{2,1,0:T(8,128)} copy(f32[2,64,640]{2,1,0:T(8,128)} %shard_map.55) | data formatting | bytes 655360
where the time goes:
time: 52.7 us; the launch traced here: 52.5 us
  Pallas kernels  50.8 us (96%)
  local copies, waits for them, and re-layouts  1.72 us (3%)
    pallas_call x1, Pallas kernels, shards(): pl.pallas_call(functools.partial(kernel, n, m), out_shape=jax.ShapeDtypeS...  50.8 us
    unnamed x1, local copies, waits for them, and re-layouts  1.72 us

commit v1 on v0

v1 whole, which is shorter than its diff:
```python
import functools

import jax
import jax.numpy as jnp
from jax import lax
from jax.experimental import pallas as pl
from jax.experimental.pallas import tpu as pltpu
from jax.sharding import PartitionSpec as P

MESH = pl.DeviceIdType.MESH
F32 = jnp.float32
BF16 = jnp.bfloat16


def dot_t(a, b):
    return lax.dot_general(a, b, (((1,), (1,)), ((), ())), preferred_element_type=F32)


def terms(x):
    first = x.astype(BF16)
    rest = x - first.astype(F32)
    second = rest.astype(BF16)
    third = (rest - second.astype(F32)).astype(BF16)
    return first, second, third


def split_dot_t(x, low):
    rows = x.shape[0]
    product = dot_t(jnp.concatenate(terms(x), axis=0), low)
    return (product[2 * rows:] + product[rows:2 * rows]) + product[:rows]


def wide(parts):
    a1, a2, a3 = parts
    return jnp.concatenate([a3, a2, a1, a2, a1, a1], axis=1)


def tall(parts, axis):
    b1, b2, b3 = parts
    return jnp.concatenate([b1, b2, b3, b1, b2, b1], axis=axis)


def exact_dot(a, b):
    return jnp.dot(wide(terms(a)), tall(terms(b), 0), preferred_element_type=F32)


def exact_dot_t(a, b):
    return dot_t(wide(terms(a)), tall(terms(b), 1))


def kernel(
    n, m, rhs_hbm, binv_hbm, entry_hbm, exit_hbm, prev_hbm, out_ref,
    rhs, binv, entry, exits, prev, arriving,
    parts, parts_in, opening, opening_in, sums, prefix, prefix_add, ahead, after,
    comp, gathered, states_out, states, forward, applied, carried, carried_in,
    carried_sum, back, back_in, local, behind_out, behind,
    local_sem, exit_sem, part_send, part_recv, sum_send, sum_recv, open_send, open_recv,
    comp_send, comp_recv, state_send, state_recv, fwd_send, fwd_recv,
    car_send, car_recv, back_send, back_recv, beh_send, beh_recv,
):
    c = lax.axis_index("chain")
    k = lax.axis_index("col")
    count, columns, width = rhs.shape
    nx = entry.shape[2]
    half = columns // 2
    window = nx + half
    chips = n // 2
    q = c // 2
    core = lax.rem(c, 2)
    mids = (m // 2 - 1, m // 2)
    blocks = 2 * count
    h = jnp.clip(k - mids[0], 0, 1)
    is_hub = (core == 1) & (k >= mids[0]) & (k <= mids[1])
    unsent = []

    def hub(side):
        return {"chain": 2 * q + 1, "col": mids[0] + side}

    def is_side(side):
        return (core == 1) & (k == mids[side])

    def remote(src, dst, send, recv, where):
        return pltpu.make_async_remote_copy(
            src_ref=src, dst_ref=dst, send_sem=send, recv_sem=recv,
            device_id=where, device_id_type=MESH,
        )

    def send(condition, *args):
        @pl.when(condition)
        def _():
            remote(*args).start()

        unsent.append((condition, args))

    here = {"chain": c, "col": k}
    loads = [
        pltpu.make_async_copy(exit_hbm, exits, local_sem.at[0]),
        pltpu.make_async_copy(entry_hbm, entry, local_sem.at[1]),
        pltpu.make_async_copy(rhs_hbm, rhs, local_sem.at[2]),
        pltpu.make_async_copy(prev_hbm, prev, local_sem.at[3]),
    ] + [
        pltpu.make_async_copy(binv_hbm.at[p], binv.at[p], local_sem.at[4 + p])
        for p in range(count)
    ]
    for load in loads:
        load.start()

    barrier = pltpu.get_barrier_semaphore()
    for d in range(1, m):
        for other in range(2):
            pl.semaphore_signal(
                barrier, 1, device_id={"chain": 2 * q + other, "col": lax.rem(k + d, m)},
                device_id_type=MESH,
            )
    pl.semaphore_signal(barrier, 1, device_id={"chain": 2 * q + 1 - core}, device_id_type=MESH)

    beside = c + 2 * core - 1
    has_beside = (beside >= 0) & (beside < n)

    @pl.when(has_beside)
    def _():
        pl.semaphore_signal(barrier, 1, device_id={"chain": beside}, device_id_type=MESH)

    @pl.when(is_hub)
    def _():
        for d in range(1, chips):
            pl.semaphore_signal(
                barrier, 1, device_id={"chain": 2 * lax.rem(q + d, chips) + 1},
                device_id_type=MESH,
            )

    @pl.when(c == n - 1)
    def _():
        arriving[...] = jnp.zeros_like(arriving)

    for load in loads[:4]:
        load.wait()

    @pl.when(c == 0)
    def _():
        opening[...] = jnp.dot(prev[...], exits[0], preferred_element_type=F32)

    def following(p):
        return exits[p + 1] if p + 1 < count else arriving[...]

    def part(p):
        after_p = following(p)
        source = jnp.dot(rhs[p], after_p, preferred_element_type=F32)
        parts[p, :half] = source[:half]
        parts[p, half:window] = -lax.dot_general(
            entry[p], after_p, (((0,), (0,)), ((), ())), preferred_element_type=F32
        )
        parts[p, window:] = source[half:]

    for p in range(count - 1):
        part(p)

    expected = 2 * m - 1 + jnp.where(has_beside, 1, 0) + jnp.where(is_hub, chips - 1, 0)
    pl.semaphore_wait(barrier, expected)

    send(c > 0, exits.at[0], arriving, exit_sem.at[0], exit_sem.at[1], {"chain": c - 1})
    for side in range(2):
        send(
            c == 0, opening.at[pl.ds(side * half, half)], opening_in.at[k],
            open_send.at[side], open_recv.at[k], hub(side),
        )

    def early_owner(j):
        return 0 if j < count else 1

    for p in range(count):
        if p + 1 == count:
            @pl.when(c < n - 1)
            def _():
                remote(
                    exits.at[0], arriving, exit_sem.at[0], exit_sem.at[1], here
                ).wait_recv()
            part(p)
        send(
            core == 0, parts.at[p], parts_in.at[0, k, p],
            part_send.at[p, 0], part_recv.at[0, k, p], hub(0),
        )
        if p + 1 < count:
            send(
                (core == 1) & jnp.logical_not(is_side(1)), parts.at[p], parts_in.at[1, k, p],
                part_send.at[p, 1], part_recv.at[1, k, p], hub(1),
            )
        else:
            for side in range(2):
                rows = pl.ds(side * half, window)
                send(
                    (core == 1) & jnp.logical_not(is_side(side)), parts.at[p, rows],
                    parts_in.at[1, k, p, rows], part_send.at[p, side],
                    part_recv.at[1, k, p], hub(side),
                )

    mine = pl.ds(pl.multiple_of(h * half, 8), window)
    yours = pl.ds(pl.multiple_of((1 - h) * half, 8), window)
    source_rows = pl.ds(pl.multiple_of(h * window, 8), half)

    def coupling(j):
        return sums[j, half:window]

    def source(j):
        return sums[j, source_rows]

    def gather_part(side, j, rows):
        owner, p = j // count, j % count
        total = None
        if owner == 1:
            total = parts[p, rows]
        for d in range(owner, m):
            other = lax.rem(mids[side] + d, m)
            remote(
                parts.at[p, rows], parts_in.at[owner, other, p, rows], part_send.at[p, 0],
                part_recv.at[owner, other, p], here,
            ).wait_recv()
            value = parts_in[owner, other, p, rows]
            total = value if total is None else total + value
        return total

    everything = pl.ds(0, nx + columns)
    for side in range(2):
        @pl.when(is_side(side))
        def _():
            for j in range(blocks - 1):
                if early_owner(j) == side:
                    sums[j] = gather_part(side, j, everything)
    for j in range(blocks - 1):
        side = early_owner(j)
        rows = pl.ds((1 - side) * half, window)
        send(
            is_side(side), sums.at[j, rows], sums.at[j, rows],
            sum_send.at[j], sum_recv.at[j], hub(1 - side),
        )

    @pl.when(is_hub)
    def _():
        for side in range(2):
            @pl.when(k == mids[side])
            def _():
                for j in range(blocks - 1):
                    if early_owner(j) != side:
                        rows = pl.ds(side * half, window)
                        remote(
                            sums.at[j, rows], sums.at[j, rows], sum_send.at[j],
                            sum_recv.at[j], here,
                        ).wait_recv()
        prefix[0] = coupling(0)
        prefix_add[0] = source(0)
        for j in range(1, blocks - 1):
            both = exact_dot(
                jnp.concatenate([prefix[j - 1], prefix_add[j - 1]], axis=0), coupling(j)
            )
            prefix[j] = both[:nx]
            prefix_add[j] = both[nx:] + source(j)

        @pl.when(q == 0)
        def _():
            total = None
            for d in range(m):
                remote(
                    opening.at[pl.ds(0, half)], opening_in.at[d], open_send.at[0],
                    open_recv.at[d], here,
                ).wait_recv()
                total = opening_in[d] if total is None else total + opening_in[d]
            states_out[0] = total

        last = blocks - 1
        for side in range(2):
            @pl.when(k == mids[side])
            def _():
                rows = pl.ds(side * half, window)
                sums[last, rows] = gather_part(side, last, rows)
        both = exact_dot(
            jnp.concatenate([prefix[last - 1], prefix_add[last - 1]], axis=0), coupling(last)
        )
        comp[:nx] = both[:nx]
        comp[nx:] = both[nx:] + source(last)

        @pl.when(q == 0)
        def _():
            comp[nx:] = exact_dot(states_out[0], comp[:nx]) + comp[nx:]

    added = pl.ds(nx, half)
    kept = pl.ds(0, nx)
    for d in range(1, chips):
        later = {"chain": 2 * lax.rem(q + d, chips) + 1}
        send(
            is_hub & (q > 0) & (q + d < chips), comp, gathered.at[q], comp_send.at[d - 1],
            comp_recv.at[q], later,
        )
        send(
            is_hub & (q == 0), comp.at[added], gathered.at[q, added], comp_send.at[d - 1],
            comp_recv.at[q], later,
        )

    @pl.when(is_hub)
    def _():
        ahead[...] = tall(
            terms(jnp.concatenate([prefix[j] for j in range(blocks - 1)], axis=1)), 0
        )

        @pl.when(q > 0)
        def _():
            remote(
                comp.at[added], gathered.at[0, added], comp_send.at[0], comp_recv.at[0], here
            ).wait_recv()

            def fold(s, state):
                remote(
                    comp, gathered.at[s], comp_send.at[0], comp_recv.at[s], here
                ).wait_recv()
                return exact_dot(state, gathered[s, :nx]) + gathered[s, nx:]

            states_out[0] = lax.fori_loop(1, q, fold, gathered[0, nx:])

        spread_out = jnp.dot(
            wide(terms(states_out[0])), ahead[...], preferred_element_type=F32
        )
        for j in range(1, blocks):
            states_out[j] = spread_out[:, (j - 1) * nx:j * nx] + prefix_add[j - 1]

    def spread(source_ref, target, sends, recvs, order):
        for p in order:
            for d in range(m):
                to = lax.rem(k + d, m)
                if d > 0:
                    send(
                        is_hub, source_ref.at[count + p], target.at[p, h],
                        sends.at[count + p, d], recvs.at[p, h], {"col": to},
                    )
                send(
                    is_hub, source_ref.at[p], target.at[p, h],
                    sends.at[p, d], recvs.at[p, h], {"chain": 2 * q, "col": to},
                )

            @pl.when(is_hub)
            def _():
                target[p, h] = source_ref[count + p]

    def arrive(target, p, recvs):
        for side in range(2):
            @pl.when(jnp.logical_not(is_side(side)))
            def _():
                remote(
                    target.at[p, side], target.at[p, side], exit_sem.at[0],
                    recvs.at[p, side], here,
                ).wait_recv()

    spread(states_out, states, state_send, state_recv, range(count))

    for d in range(1, chips):
        send(
            is_hub & (q - d >= 0), comp.at[kept], gathered.at[q, kept],
            comp_send.at[chips - 1 + d - 1], comp_recv.at[q],
            {"chain": 2 * lax.rem(q - d + chips, chips) + 1},
        )

    for p in range(count):
        arrive(states, p, state_recv)
        state = states[p].reshape(columns, nx)
        forward[k, p] = (rhs[p].astype(F32) - split_dot_t(state, entry[p])).astype(BF16)
        for way, step in ((0, 1), (1, -1)):
            beyond = k + step
            send(
                (beyond >= 0) & (beyond < m), forward.at[k, p], forward.at[k, p],
                fwd_send.at[k, p, way], fwd_recv.at[k, p], {"col": beyond},
            )

    @pl.when(is_hub)
    def _():
        suffix = [coupling(blocks - 1)]
        for j in range(blocks - 2, 0, -1):
            suffix.append(exact_dot(coupling(j), suffix[-1]))
        after[...] = tall(terms(jnp.concatenate(suffix[::-1], axis=0)), 1)

    def block(j, p):
        return binv[p, :, pl.ds(pl.multiple_of(j * width, 128), width)]

    for p in range(count):
        loads[4 + p].wait()
        applied[p] = dot_t(forward[k, p], block(k, p))
    for d in range(1, m):
        for p in range(count):
            for way, step in ((0, 1), (1, -1)):
                j = k - step * d
                beyond = k + step
                there = (j >= 0) & (j < m)

                @pl.when(there)
                def _():
                    remote(
                        forward.at[j, p], forward.at[j, p], fwd_send.at[j, p, way],
                        fwd_recv.at[j, p], here,
                    ).wait_recv()

                send(
                    there & (beyond >= 0) & (beyond < m),
                    forward.at[j, p], forward.at[j, p],
                    fwd_send.at[j, p, way], fwd_recv.at[j, p], {"col": beyond},
                )
            for step in (1, -1):
                j = k - step * d

                @pl.when((j >= 0) & (j < m))
                def _():
                    applied[p] += dot_t(forward[j, p], block(j, p))
            if d == m - 1:
                carried[p] = jnp.dot(
                    applied[p].astype(BF16), entry[p], preferred_element_type=F32
                )
                for side in range(2):
                    rows = pl.ds(side * half, half)
                    send(
                        jnp.logical_not(is_side(side)), carried.at[p, rows],
                        carried_in.at[core, k, p], car_send.at[p, side],
                        car_recv.at[core, k, p], hub(side),
                    )

    own_rows = pl.ds(pl.multiple_of(h * half, 8), half)

    @pl.when(is_hub)
    def _():
        for j in range(blocks):
            owner, p = j // count, j % count
            total = carried[p, own_rows] if owner == 1 else None
            for d in range(owner, m):
                other = lax.rem(k + d, m)
                remote(
                    carried.at[p, own_rows], carried_in.at[owner, other, p],
                    car_send.at[p, 0], car_recv.at[owner, other, p], here,
                ).wait_recv()
                value = carried_in[owner, other, p]
                total = value if total is None else total + value
            carried_sum[j] = total
        stretched = jnp.concatenate([carried_sum[j] for j in range(1, blocks)], axis=1)
        reach = jnp.concatenate([prefix[j] for j in range(blocks - 1)], axis=1)
        back[...] = exact_dot_t(stretched, reach) + carried_sum[0]

    for d in range(1, chips):
        send(
            is_hub & (q - d >= 0), back, back_in.at[q], back_send.at[d - 1],
            back_recv.at[q], {"chain": 2 * lax.rem(q - d + chips, chips) + 1},
        )

    @pl.when(is_hub)
    def _():
        local[blocks - 2] = carried_sum[blocks - 1]
        for j in range(blocks - 3, -1, -1):
            local[j] = exact_dot_t(local[j + 1], coupling(j + 2 - 1)) + carried_sum[j + 1]

        def fold(i, state):
            s = chips - 1 - i
            remote(
                comp.at[kept], gathered.at[s, kept], comp_send.at[0], comp_recv.at[s], here
            ).wait_recv()
            remote(back, back_in.at[s], back_send.at[0], back_recv.at[s], here).wait_recv()
            return exact_dot_t(state, gathered[s, :nx]) + back_in[s]

        state = lax.fori_loop(0, chips - 1 - q, fold, jnp.zeros((half, nx), F32))
        behind_out[blocks - 1] = state
        spread_out = dot_t(wide(terms(state)), after[...])
        for j in range(blocks - 1):
            behind_out[j] = spread_out[:, j * nx:(j + 1) * nx] + local[j]

    spread(behind_out, behind, beh_send, beh_recv, reversed(range(count)))

    for p in reversed(range(count)):
        arrive(behind, p, beh_recv)
        state = behind[p].reshape(columns, nx)
        out_ref[p] = applied[p] - split_dot_t(state, following(p))

    for condition, args in unsent:
        @pl.when(condition)
        def _():
            remote(*args).wait_send()


def shards(n, m, rhs, block_inverse, entry_factor, exit_factor, previous):
    count, columns, width = rhs.shape
    nx = entry_factor.shape[2]
    padded = -(-width // 128) * 128
    if padded != width:
        extra = padded - width
        rhs = jnp.pad(rhs, ((0, 0), (0, 0), (0, extra)))
        previous = jnp.pad(previous, ((0, 0), (0, extra)))
        entry_factor = jnp.pad(entry_factor, ((0, 0), (0, extra), (0, 0)))
        exit_factor = jnp.pad(exit_factor, ((0, 0), (0, extra), (0, 0)))
        block_inverse = jnp.pad(
            block_inverse.reshape(count, width, m, width),
            ((0, 0), (0, extra), (0, 0), (0, extra)),
        ).reshape(count, padded, m * padded)
    vmem = pltpu.VMEM
    dma = pltpu.SemaphoreType.DMA
    chips = n // 2
    blocks = 2 * count
    half = columns // 2
    rest = blocks - 1
    out = pl.pallas_call(
        functools.partial(kernel, n, m),
        out_shape=jax.ShapeDtypeStruct((count, columns, padded), F32),
        in_specs=[pl.BlockSpec(memory_space=pl.ANY)] * 5,
        out_specs=pl.BlockSpec(memory_space=pltpu.VMEM),
        scratch_shapes=[
            vmem((count, columns, padded), BF16),
            vmem(block_inverse.shape, BF16),
            vmem(entry_factor.shape, BF16),
            vmem(exit_factor.shape, BF16),
            vmem(previous.shape, BF16),
            vmem(exit_factor.shape[1:], BF16),
            vmem((count, nx + columns, nx), F32),
            vmem((2, m, count, nx + columns, nx), F32),
            vmem((columns, nx), F32),
            vmem((m, half, nx), F32),
            vmem((blocks, nx + columns, nx), F32),
            vmem((rest, nx, nx), F32),
            vmem((rest, half, nx), F32),
            vmem((6 * nx, rest * nx), BF16),
            vmem((rest * nx, 6 * nx), BF16),
            vmem((nx + half, nx), F32),
            vmem((chips, nx + half, nx), F32),
            vmem((blocks, half, nx), F32),
            vmem((count, 2, half, nx), F32),
            vmem((m, count, columns, padded), BF16),
            vmem((count, columns, padded), F32),
            vmem((count, columns, nx), F32),
            vmem((2, m, count, half, nx), F32),
            vmem((blocks, half, nx), F32),
            vmem((half, nx), F32),
            vmem((chips, half, nx), F32),
            vmem((rest, half, nx), F32),
            vmem((blocks, half, nx), F32),
            vmem((count, 2, half, nx), F32),
            dma((4 + count,)),
            dma((2,)),
            dma((count, 2)), dma((2, m, count)),
            dma((blocks,)), dma((blocks,)),
            dma((2,)), dma((m,)),
            dma((2 * chips,)), dma((chips,)),
            dma((blocks, m)), dma((count, 2)),
            dma((m, count, 2)), dma((m, count)),
            dma((count, 2)), dma((2, m, count)),
            dma((chips,)), dma((chips,)),
            dma((blocks, m)), dma((count, 2)),
        ],
        compiler_params=pltpu.CompilerParams(
            collective_id=0, has_side_effects=True
        ),
    )(rhs, block_inverse, entry_factor, exit_factor, previous)
    return out[:, :, :width] if padded != width else out


def solution(mesh):
    placed = (
        P("chain", None, "col"),
        P("chain", "col", None),
        P("chain", "col", None),
        P("chain", "col", None),
        P(None, "col"),
    )
    return jax.shard_map(
        functools.partial(shards, mesh.shape["chain"], mesh.shape["col"]),
        mesh=mesh, in_specs=placed, out_specs=P("chain", None, "col"), check_vma=False,
    )
```

time: 52.7 us -> 50.4 us (0.956)
  Pallas kernels: 50.8 us -> 48.5 us
    pallas_call x1, Pallas kernels: 50.8 us -> 48.5 us  [shards(): pl.pallas_call(functools.partial(kernel, n, m), out_shape=jax.ShapeDtypeS...]
where the time goes in v1:
time: 50.4 us; the launch traced here: 50.3 us
  Pallas kernels  48.5 us (96%)
  local copies, waits for them, and re-layouts  1.72 us (3%)
    pallas_call x1, Pallas kernels, shards(): pl.pallas_call(functools.partial(kernel, n, m), out_shape=jax.ShapeDtypeS...  48.5 us
    unnamed x1, local copies, waits for them, and re-layouts  1.72 us

profile of v1, /device:TPU:0, one launch (start us, length us, event | category | flops | bytes accessed | tf_op | source)
XLA Modules:
  0.0 50.3 jit_solution(15288975384437492236)
XLA Ops:
  0.0 48.5 %shard_map.55 = f32[2,64,640]{2,1,0:T(8,128)} custom-call(bf16[2,64,640]{2,1,0:T(8,128)(2,1)} %rhs_hbm.1, bf16[2,640,2560]{2,1,0:T(8,128)(2,1)} %binv_hbm.1, bf16[2,640,128]{2,1,0:T(8,128)(2,1)} %entry_hbm.1, bf16[2,640,128]{2,1,0:T(8,128)(2,1)} %exit_hbm.1, bf16[64,640]{1,0:T(8,128)(2,1)} %prev_hbm.1), custom_call_target="tpu_custom_call" | custom-call | tf_op jit(solution)/shard_map/pallas_call | solution.py:500
  48.5 1.7 %copy.7 = f32[2,64,640]{2,1,0:T(8,128)} copy(f32[2,64,640]{2,1,0:T(8,128)} %shard_map.55) | data formatting | bytes 655360

commit v2 on v1

--- a/solution.py
+++ b/solution.py
@@ -54,7 +54,7 @@
     parts, parts_in, opening, opening_in, sums, prefix, prefix_add, ahead, after,
     comp, gathered, states_out, states, forward, applied, carried, carried_in,
     carried_sum, back, back_in, local, behind_out, behind,
-    local_sem, exit_sem, part_send, part_recv, sum_send, sum_recv, open_send, open_recv,
+    local_sem, exit_sem, part_send, part_recv, open_send, open_recv,
     comp_send, comp_recv, state_send, state_recv, fwd_send, fwd_recv,
     car_send, car_recv, back_send, back_recv, beh_send, beh_recv,
 ):
@@ -77,7 +77,10 @@
         return {"chain": 2 * q + 1, "col": mids[0] + side}
 
     def is_side(side):
-        return (core == 1) & (k == mids[side])
+        return (core == 1) & (k == mids[0] + side)
+
+    low = jnp.where(k <= mids[0], 1, 0)
+    far_first = (low, 1 - low)
 
     def remote(src, dst, send, recv, where):
         return pltpu.make_async_remote_copy(
@@ -165,9 +168,6 @@
             open_send.at[side], open_recv.at[k], hub(side),
         )
 
-    def early_owner(j):
-        return 0 if j < count else 1
-
     for p in range(count):
         if p + 1 == count:
             @pl.when(c < n - 1)
@@ -176,26 +176,15 @@
                     exits.at[0], arriving, exit_sem.at[0], exit_sem.at[1], here
                 ).wait_recv()
             part(p)
-        send(
-            core == 0, parts.at[p], parts_in.at[0, k, p],
-            part_send.at[p, 0], part_recv.at[0, k, p], hub(0),
-        )
-        if p + 1 < count:
+        for side in far_first:
+            rows = pl.ds(pl.multiple_of(side * half, 8), window)
             send(
-                (core == 1) & jnp.logical_not(is_side(1)), parts.at[p], parts_in.at[1, k, p],
-                part_send.at[p, 1], part_recv.at[1, k, p], hub(1),
+                jnp.logical_not(is_side(side)), parts.at[p, rows],
+                parts_in.at[core, k, p, rows], part_send.at[p, side],
+                part_recv.at[core, k, p], hub(side),
             )
-        else:
-            for side in range(2):
-                rows = pl.ds(side * half, window)
-                send(
-                    (core == 1) & jnp.logical_not(is_side(side)), parts.at[p, rows],
-                    parts_in.at[1, k, p, rows], part_send.at[p, side],
-                    part_recv.at[1, k, p], hub(side),
-                )
 
     mine = pl.ds(pl.multiple_of(h * half, 8), window)
-    yours = pl.ds(pl.multiple_of((1 - h) * half, 8), window)
     source_rows = pl.ds(pl.multiple_of(h * window, 8), half)
 
     def coupling(j):
@@ -204,51 +193,26 @@
     def source(j):
         return sums[j, source_rows]
 
-    def gather_part(side, j, rows):
+    def gather_part(j):
         owner, p = j // count, j % count
-        total = None
-        if owner == 1:
-            total = parts[p, rows]
+        total = parts[p, mine] if owner == 1 else None
         for d in range(owner, m):
-            other = lax.rem(mids[side] + d, m)
+            other = lax.rem(k + d, m)
             remote(
-                parts.at[p, rows], parts_in.at[owner, other, p, rows], part_send.at[p, 0],
+                parts.at[p, mine], parts_in.at[owner, other, p, mine], part_send.at[p, 0],
                 part_recv.at[owner, other, p], here,
             ).wait_recv()
-            value = parts_in[owner, other, p, rows]
+            value = parts_in[owner, other, p, mine]
             total = value if total is None else total + value
-        return total
-
-    everything = pl.ds(0, nx + columns)
-    for side in range(2):
-        @pl.when(is_side(side))
-        def _():
-            for j in range(blocks - 1):
-                if early_owner(j) == side:
-                    sums[j] = gather_part(side, j, everything)
-    for j in range(blocks - 1):
-        side = early_owner(j)
-        rows = pl.ds((1 - side) * half, window)
-        send(
-            is_side(side), sums.at[j, rows], sums.at[j, rows],
-            sum_send.at[j], sum_recv.at[j], hub(1 - side),
-        )
+        sums[j, mine] = total
 
     @pl.when(is_hub)
     def _():
-        for side in range(2):
-            @pl.when(k == mids[side])
-            def _():
-                for j in range(blocks - 1):
-                    if early_owner(j) != side:
-                        rows = pl.ds(side * half, window)
-                        remote(
-                            sums.at[j, rows], sums.at[j, rows], sum_send.at[j],
-                            sum_recv.at[j], here,
-                        ).wait_recv()
+        gather_part(0)
         prefix[0] = coupling(0)
         prefix_add[0] = source(0)
         for j in range(1, blocks - 1):
+            gather_part(j)
             both = exact_dot(
                 jnp.concatenate([prefix[j - 1], prefix_add[j - 1]], axis=0), coupling(j)
             )
@@ -267,11 +231,7 @@
             states_out[0] = total
 
         last = blocks - 1
-        for side in range(2):
-            @pl.when(k == mids[side])
-            def _():
-                rows = pl.ds(side * half, window)
-                sums[last, rows] = gather_part(side, last, rows)
+        gather_part(last)
         both = exact_dot(
             jnp.concatenate([prefix[last - 1], prefix_add[last - 1]], axis=0), coupling(last)
         )
@@ -410,8 +370,8 @@
                 carried[p] = jnp.dot(
                     applied[p].astype(BF16), entry[p], preferred_element_type=F32
                 )
-                for side in range(2):
-                    rows = pl.ds(side * half, half)
+                for side in far_first:
+                    rows = pl.ds(pl.multiple_of(side * half, 8), half)
                     send(
                         jnp.logical_not(is_side(side)), carried.at[p, rows],
                         carried_in.at[core, k, p], car_send.at[p, side],
@@ -448,7 +408,7 @@
     def _():
         local[blocks - 2] = carried_sum[blocks - 1]
         for j in range(blocks - 3, -1, -1):
-            local[j] = exact_dot_t(local[j + 1], coupling(j + 2 - 1)) + carried_sum[j + 1]
+            local[j] = exact_dot_t(local[j + 1], coupling(j + 1)) + carried_sum[j + 1]
 
         def fold(i, state):
             s = chips - 1 - i
@@ -499,8 +459,8 @@
     rest = blocks - 1
     out = pl.pallas_call(
         functools.partial(kernel, n, m),
-        out_shape=jax.ShapeDtypeStruct((count, columns, padded), F32),
-        in_specs=[pl.BlockSpec(memory_space=pl.ANY)] * 5,
+        out_shape=pltpu.VMEM((count, columns, padded), F32),
+        in_specs=[pl.BlockSpec(memory_space=pltpu.HBM)] * 5,
         out_specs=pl.BlockSpec(memory_space=pltpu.VMEM),
         scratch_shapes=[
             vmem((count, columns, padded), BF16),
@@ -535,7 +495,6 @@
             dma((4 + count,)),
             dma((2,)),
             dma((count, 2)), dma((2, m, count)),
-            dma((blocks,)), dma((blocks,)),
             dma((2,)), dma((m,)),
             dma((2 * chips,)), dma((chips,)),
             dma((blocks, m)), dma((count, 2)),
@@ -545,9 +504,12 @@
             dma((blocks, m)), dma((count, 2)),
         ],
         compiler_params=pltpu.CompilerParams(
-            collective_id=0, has_side_effects=True
+            collective_id=0, has_side_effects=True, vmem_limit_bytes=40 * 2**20
         ),
-    )(rhs, block_inverse, entry_factor, exit_factor, previous)
+    )(*(
+        pltpu.with_memory_space_constraint(x, pltpu.HBM)
+        for x in (rhs, block_inverse, entry_factor, exit_factor, previous)
+    ))
     return out[:, :, :width] if padded != width else out
 
 

time: 50.4 us -> 46.3 us (0.919)
  Pallas kernels: 48.5 us -> 45.5 us
  local copies, waits for them, and re-layouts: 1.72 us -> 0.73 us
    pallas_call x1, Pallas kernels: 48.5 us -> 45.5 us  [shards(): pl.pallas_call(functools.partial(kernel, n, m), out_shape=pltpu.VMEM((cou...]
    unnamed x1, local copies, waits for them, and re-layouts: 1.72 us -> 0.73 us
where the time goes in v2:
time: 46.3 us; the launch traced here: 46.2 us
  Pallas kernels  45.5 us (98%)
  local copies, waits for them, and re-layouts  0.73 us (2%)
    pallas_call x1, Pallas kernels, shards(): pl.pallas_call(functools.partial(kernel, n, m), out_shape=pltpu.VMEM((cou...  45.5 us

profile of v2, /device:TPU:0, one launch (start us, length us, event | category | flops | bytes accessed | tf_op | source)
XLA Modules:
  0.0 46.2 jit_solution(1959680921706546745)
XLA Ops:
  0.0 45.5 %shard_map.55 = f32[2,64,640]{2,1,0:T(8,128)S(1)} custom-call(bf16[2,64,640]{2,1,0:T(8,128)(2,1)} %rhs_hbm.1, bf16[2,640,2560]{2,1,0:T(8,128)(2,1)} %binv_hbm.1, bf16[2,640,128]{2,1,0:T(8,128)(2,1)} %entry_hbm.1, bf16[2,640,128]{2,1,0:T(8,128)(2,1)} %exit_hbm.1, bf16[64,640]{1,0:T(8,128)(2,1)} %prev_hbm.1), custom_call_target="tpu_custom_call" | custom-call | tf_op jit(solution)/shard_map/pallas_call | solution.py:460
  45.5 0.7 %copy.7 = f32[2,64,640]{2,1,0:T(8,128)} copy(f32[2,64,640]{2,1,0:T(8,128)S(1)} %shard_map.55) | data formatting | bytes 655360

commit v3 on v2

v3 whole, which is shorter than its diff:
```python
import functools

import jax
import jax.numpy as jnp
from jax import lax
from jax.experimental import pallas as pl
from jax.experimental.pallas import tpu as pltpu
from jax.sharding import PartitionSpec as P

MESH = pl.DeviceIdType.MESH
F32 = jnp.float32
BF16 = jnp.bfloat16


def dot_t(a, b):
    return lax.dot_general(a, b, (((1,), (1,)), ((), ())), preferred_element_type=F32)


def terms(x):
    first = x.astype(BF16)
    rest = x - first.astype(F32)
    second = rest.astype(BF16)
    third = (rest - second.astype(F32)).astype(BF16)
    return first, second, third


def split_dot_t(x, low):
    rows = x.shape[0]
    product = dot_t(jnp.concatenate(terms(x), axis=0), low)
    return (product[2 * rows:] + product[rows:2 * rows]) + product[:rows]


def wide(parts):
    a1, a2, a3 = parts
    return jnp.concatenate([a3, a2, a1, a2, a1, a1], axis=1)


def tall(parts, axis):
    b1, b2, b3 = parts
    return jnp.concatenate([b1, b2, b3, b1, b2, b1], axis=axis)


def exact_dot(a, b):
    return jnp.dot(wide(terms(a)), tall(terms(b), 0), preferred_element_type=F32)


def exact_dot_t(a, b):
    return dot_t(wide(terms(a)), tall(terms(b), 1))


def prepared(ref, b):
    for i, term in enumerate(terms(b)):
        ref[i] = term


def stacked(a, b1, b2, b3, product):
    rows = a.shape[0]
    a1, a2, a3 = terms(a)
    y1 = product(jnp.concatenate([a1, a2, a3], axis=0), b1)
    y2 = product(jnp.concatenate([a1, a2], axis=0), b2)
    y3 = product(a1, b3)
    small = (y1[2 * rows:] + y2[rows:]) + y3
    return (small + (y1[rows:2 * rows] + y2[:rows])) + y1[:rows]


def plain(a, b):
    return jnp.dot(a, b, preferred_element_type=F32)


def kernel(
    n, m, rhs_hbm, binv_hbm, entry_hbm, exit_hbm, prev_hbm, out_ref,
    rhs, binv, entry, exits, prev, arriving,
    parts, parts_in, opening, opening_in, sums, prefix, prefix_add, ahead, reach, reach_terms,
    comp, gathered, states_out, states, forward, applied, carried, carried_in,
    carried_sum, back, back_in, behind_out, behind, near_entry, near_rhs,
    local_sem, exit_sem, part_send, part_recv, open_send, open_recv,
    comp_send, comp_recv, state_send, state_recv, fwd_send, fwd_recv,
    car_send, car_recv, back_send, back_recv, beh_send, beh_recv, near_send, near_recv,
):
    c = lax.axis_index("chain")
    k = lax.axis_index("col")
    count, columns, width = rhs.shape
    nx = entry.shape[2]
    half = columns // 2
    window = nx + half
    chips = n // 2
    q = c // 2
    core = lax.rem(c, 2)
    mids = (m // 2 - 1, m // 2)
    blocks = 2 * count
    rest = blocks - 1
    h = jnp.clip(k - mids[0], 0, 1)
    is_hub = (core == 1) & (k >= mids[0]) & (k <= mids[1])
    unsent = []

    def hub(side):
        return {"chain": 2 * q + 1, "col": mids[0] + side}

    def is_side(side):
        return (core == 1) & (k == mids[0] + side)

    low = jnp.where(k <= mids[0], 1, 0)
    far_first = (low, 1 - low)

    def remote(src, dst, send, recv, where):
        return pltpu.make_async_remote_copy(
            src_ref=src, dst_ref=dst, send_sem=send, recv_sem=recv,
            device_id=where, device_id_type=MESH,
        )

    def send(condition, *args):
        @pl.when(condition)
        def _():
            remote(*args).start()

    def sent(condition, ref, semaphore):
        unsent.append((condition, ref, semaphore))

    def received(ref, semaphore):
        remote(ref, ref, exit_sem.at[0], semaphore, here).wait_recv()

    here = {"chain": c, "col": k}
    loads = [
        pltpu.make_async_copy(exit_hbm, exits, local_sem.at[0]),
        pltpu.make_async_copy(entry_hbm, entry, local_sem.at[1]),
        pltpu.make_async_copy(rhs_hbm, rhs, local_sem.at[2]),
        pltpu.make_async_copy(prev_hbm, prev, local_sem.at[3]),
    ] + [
        pltpu.make_async_copy(binv_hbm.at[p], binv.at[p], local_sem.at[4 + p])
        for p in range(count)
    ]
    for load in loads[:4]:
        load.start()

    barrier = pltpu.get_barrier_semaphore()
    for d in range(1, m):
        for other in range(2):
            pl.semaphore_signal(
                barrier, 1, device_id={"chain": 2 * q + other, "col": lax.rem(k + d, m)},
                device_id_type=MESH,
            )
    pl.semaphore_signal(barrier, 1, device_id={"chain": 2 * q + 1 - core}, device_id_type=MESH)

    beside = c + 2 * core - 1
    has_beside = (beside >= 0) & (beside < n)

    @pl.when(has_beside)
    def _():
        pl.semaphore_signal(barrier, 1, device_id={"chain": beside}, device_id_type=MESH)

    @pl.when(is_hub)
    def _():
        for d in range(1, chips):
            pl.semaphore_signal(
                barrier, 1, device_id={"chain": 2 * lax.rem(q + d, chips) + 1},
                device_id_type=MESH,
            )

    @pl.when(c == n - 1)
    def _():
        arriving[...] = jnp.zeros_like(arriving)

    for load in loads[:4]:
        load.wait()
    for load in loads[4:]:
        load.start()

    @pl.when(c == 0)
    def _():
        opening[...] = jnp.dot(prev[...], exits[0], preferred_element_type=F32)

    def following(p):
        return exits[p + 1] if p + 1 < count else arriving[...]

    def part(p):
        after_p = following(p)
        source = jnp.dot(rhs[p], after_p, preferred_element_type=F32)
        parts[p, :half] = source[:half]
        parts[p, half:window] = -lax.dot_general(
            entry[p], after_p, (((0,), (0,)), ((), ())), preferred_element_type=F32
        )
        parts[p, window:] = source[half:]

    for p in range(count - 1):
        part(p)

    expected = 2 * m - 1 + jnp.where(has_beside, 1, 0) + jnp.where(is_hub, chips - 1, 0)
    pl.semaphore_wait(barrier, expected)

    send(c > 0, exits.at[0], arriving, exit_sem.at[0], exit_sem.at[1], {"chain": c - 1})
    sent(c > 0, arriving, exit_sem.at[0])
    for side in range(2):
        send(
            c == 0, opening.at[pl.ds(side * half, half)], opening_in.at[k],
            open_send, open_recv, hub(side),
        )
    sent(c == 0, opening, open_send)

    for p in range(count):
        if p + 1 == count:
            @pl.when(c < n - 1)
            def _():
                received(arriving, exit_sem.at[1])
            part(p)
        for side in far_first:
            rows = pl.ds(pl.multiple_of(side * half, 8), window)
            send(
                jnp.logical_not(is_side(side)), parts.at[p, rows],
                parts_in.at[core, k, p, rows], part_send,
                part_recv.at[core * count + p], hub(side),
            )
    sent(jnp.logical_not(is_hub), parts_in.at[0, pl.ds(0, 2), :, pl.ds(0, window)], part_send)
    sent(is_hub, parts_in.at[0, 0, :, pl.ds(0, window)], part_send)

    is_end = (k == 0) | (k == m - 1)
    for way, (at, to) in enumerate(((m - 2, m - 1), (1, 0))):
        send(k == at, entry, near_entry, near_send.at[way, 0], near_recv.at[0], {"col": to})
        send(k == at, rhs, near_rhs, near_send.at[way, 1], near_recv.at[1], {"col": to})
        sent(k == at, entry, near_send.at[way, 0])
        sent(k == at, rhs, near_send.at[way, 1])

    mine = pl.ds(pl.multiple_of(h * half, 8), window)
    source_rows = pl.ds(pl.multiple_of(h * window, 8), half)

    def coupling(j):
        return sums[j, half:window]

    def source(j):
        return sums[j, source_rows]

    def gather_part(j):
        owner, p = j // count, j % count
        received(parts_in.at[owner, pl.ds(0, m - owner), p, mine], part_recv.at[j])
        total = parts[p, mine] if owner == 1 else None
        for d in range(owner, m):
            value = parts_in[owner, lax.rem(k + d, m), p, mine]
            total = value if total is None else total + value
        sums[j, mine] = total

    @pl.when(is_hub)
    def _():
        gather_part(0)
        prefix[0] = coupling(0)
        prefix_add[0] = source(0)
        for j in range(1, blocks - 1):
            gather_part(j)
            both = exact_dot(
                jnp.concatenate([prefix[j - 1], prefix_add[j - 1]], axis=0), coupling(j)
            )
            prefix[j] = both[:nx]
            prefix_add[j] = both[nx:] + source(j)

        @pl.when(q == 0)
        def _():
            received(opening_in, open_recv)
            total = opening_in[0]
            for d in range(1, m):
                total += opening_in[d]
            states_out[0] = total

        last = blocks - 1
        gather_part(last)
        both = exact_dot(
            jnp.concatenate([prefix[last - 1], prefix_add[last - 1]], axis=0), coupling(last)
        )
        comp[:nx] = both[:nx]
        comp[nx:] = both[nx:] + source(last)

        @pl.when(q == 0)
        def _():
            comp[nx:] = exact_dot(states_out[0], comp[:nx]) + comp[nx:]

    added = pl.ds(nx, half)
    kept = pl.ds(0, nx)
    for d in range(1, chips):
        to = lax.rem(q + d, chips)
        later = {"chain": 2 * to + 1}
        send(
            is_hub & (q > 0) & (q + d < chips), comp, gathered.at[q], comp_send.at[to],
            comp_recv.at[q], later,
        )
        sent(is_hub & (q > 0) & (q + d < chips), comp, comp_send.at[to])
        send(
            is_hub & (q == 0), comp.at[added], gathered.at[q, added], comp_send.at[to],
            comp_recv.at[q], later,
        )
        sent(is_hub & (q == 0), comp.at[added], comp_send.at[to])

    @pl.when(is_hub)
    def _():
        prepared(ahead, jnp.concatenate([prefix[j] for j in range(blocks - 1)], axis=1))

        @pl.when(q > 0)
        def _():
            received(gathered.at[0, added], comp_recv.at[0])

            def fold(s, state):
                received(gathered.at[s], comp_recv.at[s])
                return exact_dot(state, gathered[s, :nx]) + gathered[s, nx:]

            states_out[0] = lax.fori_loop(1, q, fold, gathered[0, nx:])

        spread_out = stacked(states_out[0], ahead[0], ahead[1], ahead[2], plain)
        for j in range(1, blocks):
            states_out[j] = spread_out[:, (j - 1) * nx:j * nx] + prefix_add[j - 1]

    def spread(source_ref, target, sends, recvs, order):
        for p in order:
            for i in range(m):
                to = jnp.where(h == 0, m - 1 - i, i)
                send(
                    is_hub, source_ref.at[p], target.at[p, h],
                    sends.at[0], recvs.at[p], {"chain": 2 * q, "col": to},
                )
                send(
                    is_hub & (to != k), source_ref.at[count + p], target.at[p, h],
                    sends.at[1], recvs.at[p], {"col": to},
                )

            @pl.when(is_hub)
            def _():
                target[p, h] = source_ref[count + p]

        sent(is_hub, carried_in.at[0, pl.ds(0, m - 1)], sends.at[1])
        sent(is_hub, carried_in.at[0], sends.at[0])

    def arrive(target, p, recvs):
        @pl.when(is_hub)
        def _():
            received(target.at[p, 0], recvs.at[p])

        @pl.when(jnp.logical_not(is_hub))
        def _():
            received(target.at[p], recvs.at[p])

    spread(states_out, states, state_send, state_recv, range(count))

    for d in range(1, chips):
        to = lax.rem(q - d + chips, chips)
        send(
            is_hub & (q - d >= 0), comp.at[kept], gathered.at[q, kept],
            comp_send.at[to], comp_recv.at[q], {"chain": 2 * to + 1},
        )
        sent(is_hub & (q - d >= 0), comp.at[kept], comp_send.at[to])

    halves = [pl.ds(side * half, half) for side in range(2)]

    def leave(p, condition):
        for way, step in ((0, 1), (1, -1)):
            beyond = k + step
            goes = (beyond >= 0) & (beyond < m) & jnp.logical_not(is_last(beyond))
            for side, rows in enumerate(halves):
                send(
                    goes & condition, forward.at[k, p, rows], forward.at[k, p, rows],
                    fwd_send.at[way], fwd_recv.at[k, p, side], {"col": beyond},
                )

    def is_last(position):
        return (position == 0) | (position == m - 1)

    for place in range(m):
        for way in range(2):
            last = (m - 1, 0)[way]
            if place == last:
                continue
            passed = (place + 1, m - place)[way]
            beside_last = abs(place - last) == 1
            if m > 3 and False:
                for side in range(2):
                    amount = passed - beside_last
                    if side == 0:
                        amount += (passed == 1) - (passed == m - 1)
                    if amount > 0:
                        sent(
                            (k == place) & (core == side), forward.at[pl.ds(0, amount)],
                            fwd_send.at[way],
                        )
            elif passed > beside_last:
                sent(k == place, forward.at[pl.ds(0, passed - beside_last)], fwd_send.at[way])

    for p in range(count):
        arrive(states, p, state_recv)
        state = states[p].reshape(columns, nx)
        forward[k, p] = (rhs[p].astype(F32) - split_dot_t(state, entry[p])).astype(BF16)
        leave(p, core == 0)

    def block(j, p):
        return binv[p, :, pl.ds(pl.multiple_of(j * width, 128), width)]

    for p in range(count):
        loads[4 + p].wait()
        applied[p] = dot_t(forward[k, p], block(k, p))
        leave(p, core == 1)
    near = jnp.where(k == 0, 1, m - 2)

    @pl.when(is_end)
    def _():
        received(near_entry, near_recv.at[0])
        received(near_rhs, near_recv.at[1])
        for p in range(count):
            state = states[p].reshape(columns, nx)
            near_block = near_rhs[p].astype(F32) - split_dot_t(state, near_entry[p])
            applied[p] += dot_t(near_block.astype(BF16), block(near, p))

    def come(d, p):
        for side, rows in enumerate(halves):
            for way, step in ((0, 1), (1, -1)):
                j = k - step * d
                beyond = k + step
                there = (j >= 0) & (j < m)
                if d == 1:
                    there &= jnp.logical_not(is_last(k))

                @pl.when(there)
                def _():
                    received(forward.at[j, p, rows], fwd_recv.at[j, p, side])

                if d + 1 < m:
                    send(
                        there & (beyond >= 0) & (beyond < m),
                        forward.at[j, p, rows], forward.at[j, p, rows],
                        fwd_send.at[way], fwd_recv.at[j, p, side], {"col": beyond},
                    )

    for d in range(1, m - 1):
        for p in range(count):
            come(d, p)
    for d in range(1, m):
        for p in range(count):
            if d + 1 == m:
                come(d, p)
            for step in (1, -1):
                j = k - step * d
                there = (j >= 0) & (j < m)
                if d == 1:
                    there &= jnp.logical_not(is_last(k))

                @pl.when(there)
                def _():
                    applied[p] += dot_t(forward[j, p], block(j, p))
            if d == m - 1:
                carried[p] = jnp.dot(
                    applied[p].astype(BF16), entry[p], preferred_element_type=F32
                )
                for side in far_first:
                    rows = pl.ds(pl.multiple_of(side * half, 8), half)
                    send(
                        jnp.logical_not(is_side(side)), carried.at[p, rows],
                        carried_in.at[core, k, p], car_send,
                        car_recv.at[core * count + p], hub(side),
                    )
    sent(jnp.logical_not(is_hub), carried_in.at[0, pl.ds(0, 2)], car_send)
    sent(is_hub, carried_in.at[0, 0], car_send)

    own_rows = pl.ds(pl.multiple_of(h * half, 8), half)

    @pl.when(is_hub)
    def _():
        suffix = [coupling(blocks - 1)]
        for j in range(blocks - 2, 0, -1):
            suffix.append(exact_dot(coupling(j), suffix[-1]))
        same = lax.broadcasted_iota(jnp.int32, (nx, nx), 0) == lax.broadcasted_iota(
            jnp.int32, (nx, nx), 1
        )
        reach[...] = jnp.concatenate(suffix[::-1] + [jnp.where(same, 1.0, 0.0)], axis=0)

        def extend(s, carry):
            at = pl.ds(pl.multiple_of((s - 1) * nx, 128), nx)
            for i, term in enumerate(terms(reach[...])):
                reach_terms[i, :, at] = term
            received(gathered.at[s, kept], comp_recv.at[s])
            reach[...] = exact_dot(reach[...], gathered[s, :nx])
            return carry

        reach_terms[...] = jnp.zeros_like(reach_terms)
        lax.fori_loop(q + 1, chips, extend, 0)

    @pl.when(is_hub)
    def _():
        offset = None
        for p in range(count):
            for owner in (1, 0):
                j = owner * count + p
                received(carried_in.at[owner, pl.ds(0, m - owner), p], car_recv.at[j])
                total = carried[p, own_rows] if owner == 1 else None
                for d in range(owner, m):
                    value = carried_in[owner, lax.rem(k + d, m), p]
                    total = value if total is None else total + value
                carried_sum[j] = total
                if j > 0:
                    at = slice((j - 1) * nx, j * nx)
                    total = stacked(
                        total, ahead[0, :, at], ahead[1, :, at], ahead[2, :, at], dot_t
                    )
                offset = total if offset is None else offset + total
        back[...] = offset

    for d in range(1, chips):
        to = lax.rem(q - d + chips, chips)
        send(
            is_hub & (q - d >= 0), back, back_in.at[q], back_send.at[d - 1],
            back_recv.at[q], {"chain": 2 * to + 1},
        )
        sent(is_hub & (q - d >= 0), back, back_send.at[d - 1])

    @pl.when(is_hub)
    def _():
        behind_out[blocks - 1] = jnp.zeros((half, nx), F32)
        behind_out[blocks - 2] = carried_sum[blocks - 1]
        for j in range(blocks - 3, -1, -1):
            behind_out[j] = exact_dot_t(behind_out[j + 1], coupling(j + 1)) + carried_sum[j + 1]

        for s in range(1, chips):
            @pl.when(s > q)
            def _():
                received(back_in.at[s], back_recv.at[s])

            @pl.when(s <= q)
            def _():
                back_in[s] = jnp.zeros((half, nx), F32)

        more = stacked(
            jnp.concatenate([back_in[s] for s in range(1, chips)], axis=1),
            reach_terms[0], reach_terms[1], reach_terms[2], dot_t,
        )
        for j in range(blocks):
            behind_out[j] += more[:, j * nx:(j + 1) * nx]

    spread(behind_out, behind, beh_send, beh_recv, reversed(range(count)))

    for p in reversed(range(count)):
        arrive(behind, p, beh_recv)
        state = behind[p].reshape(columns, nx)
        out_ref[p] = applied[p] - split_dot_t(state, following(p))

    for condition, ref, semaphore in unsent:
        @pl.when(condition)
        def _():
            remote(ref, ref, semaphore, semaphore, here).wait_send()


def shards(n, m, rhs, block_inverse, entry_factor, exit_factor, previous):
    count, columns, width = rhs.shape
    nx = entry_factor.shape[2]
    padded = -(-width // 128) * 128
    if padded != width:
        extra = padded - width
        rhs = jnp.pad(rhs, ((0, 0), (0, 0), (0, extra)))
        previous = jnp.pad(previous, ((0, 0), (0, extra)))
        entry_factor = jnp.pad(entry_factor, ((0, 0), (0, extra), (0, 0)))
        exit_factor = jnp.pad(exit_factor, ((0, 0), (0, extra), (0, 0)))
        block_inverse = jnp.pad(
            block_inverse.reshape(count, width, m, width),
            ((0, 0), (0, extra), (0, 0), (0, extra)),
        ).reshape(count, padded, m * padded)
    vmem = pltpu.VMEM
    dma = pltpu.SemaphoreType.DMA
    chips = n // 2
    blocks = 2 * count
    half = columns // 2
    rest = blocks - 1
    out = pl.pallas_call(
        functools.partial(kernel, n, m),
        out_shape=pltpu.VMEM((count, columns, padded), F32),
        in_specs=[pl.BlockSpec(memory_space=pltpu.HBM)] * 5,
        out_specs=pl.BlockSpec(memory_space=pltpu.VMEM),
        scratch_shapes=[
            vmem((count, columns, padded), BF16),
            vmem(block_inverse.shape, BF16),
            vmem(entry_factor.shape, BF16),
            vmem(exit_factor.shape, BF16),
            vmem(previous.shape, BF16),
            vmem(exit_factor.shape[1:], BF16),
            vmem((count, nx + columns, nx), F32),
            vmem((2, m, count, nx + columns, nx), F32),
            vmem((columns, nx), F32),
            vmem((m, half, nx), F32),
            vmem((blocks, nx + columns, nx), F32),
            vmem((rest, nx, nx), F32),
            vmem((rest, half, nx), F32),
            vmem((3, nx, rest * nx), BF16),
            vmem((blocks * nx, nx), F32),
            vmem((3, blocks * nx, (chips - 1) * nx), BF16),
            vmem((nx + half, nx), F32),
            vmem((chips, nx + half, nx), F32),
            vmem((blocks, half, nx), F32),
            vmem((count, 2, half, nx), F32),
            vmem((m, count, columns, padded), BF16),
            vmem((count, columns, padded), F32),
            vmem((count, columns, nx), F32),
            vmem((2, m, count, half, nx), F32),
            vmem((blocks, half, nx), F32),
            vmem((half, nx), F32),
            vmem((chips, half, nx), F32),
            vmem((blocks, half, nx), F32),
            vmem((count, 2, half, nx), F32),
            vmem(entry_factor.shape, BF16),
            vmem((count, columns, padded), BF16),
            dma((4 + count,)),
            dma((2,)),
            dma(()), dma((blocks,)),
            dma(()), dma(()),
            dma((chips,)), dma((chips,)),
            dma((2,)), dma((count,)),
            dma((2,)), dma((m, count, 2)),
            dma(()), dma((blocks,)),
            dma((chips - 1,)), dma((chips,)),
            dma((2,)), dma((count,)),
            dma((2, 2)), dma((2,)),
        ],
        compiler_params=pltpu.CompilerParams(
            collective_id=0, has_side_effects=True, vmem_limit_bytes=40 * 2**20
        ),
    )(*(
        pltpu.with_memory_space_constraint(x, pltpu.HBM)
        for x in (rhs, block_inverse, entry_factor, exit_factor, previous)
    ))
    return out[:, :, :width] if padded != width else out


def solution(mesh):
    placed = (
        P("chain", None, "col"),
        P("chain", "col", None),
        P("chain", "col", None),
        P("chain", "col", None),
        P(None, "col"),
    )
    return jax.shard_map(
        functools.partial(shards, mesh.shape["chain"], mesh.shape["col"]),
        mesh=mesh, in_specs=placed, out_specs=P("chain", None, "col"), check_vma=False,
    )
```

time: 46.3 us -> 44.8 us (0.968)
  Pallas kernels: 45.5 us -> 44 us
    pallas_call x1, Pallas kernels: 45.5 us -> 44 us  [shards(): pl.pallas_call(functools.partial(kernel, n, m), out_shape=pltpu.VMEM((cou...]
where the time goes in v3:
time: 44.8 us; the launch traced here: 44.7 us
  Pallas kernels  44 us (98%)
  local copies, waits for them, and re-layouts  0.73 us (2%)
    pallas_call x1, Pallas kernels, shards(): pl.pallas_call(functools.partial(kernel, n, m), out_shape=pltpu.VMEM((cou...  44 us

profile of v3, /device:TPU:0, one launch (start us, length us, event | category | flops | bytes accessed | tf_op | source)
XLA Modules:
  0.0 44.7 jit_solution(17880241035747888372)
XLA Ops:
  0.0 44.0 %shard_map.55 = f32[2,64,640]{2,1,0:T(8,128)S(1)} custom-call(bf16[2,64,640]{2,1,0:T(8,128)(2,1)} %rhs_hbm.1, bf16[2,640,2560]{2,1,0:T(8,128)(2,1)} %binv_hbm.1, bf16[2,640,128]{2,1,0:T(8,128)(2,1)} %entry_hbm.1, bf16[2,640,128]{2,1,0:T(8,128)(2,1)} %exit_hbm.1, bf16[64,640]{1,0:T(8,128)(2,1)} %prev_hbm.1), custom_call_target="tpu_custom_call" | custom-call | tf_op jit(solution)/shard_map/pallas_call | solution.py:562
  44.0 0.7 %copy.7 = f32[2,64,640]{2,1,0:T(8,128)} copy(f32[2,64,640]{2,1,0:T(8,128)S(1)} %shard_map.55) | data formatting | bytes 655360

commit v4 on v3

--- a/solution.py
+++ b/solution.py
@@ -72,10 +72,11 @@
     rhs, binv, entry, exits, prev, arriving,
     parts, parts_in, opening, opening_in, sums, prefix, prefix_add, ahead, reach, reach_terms,
     comp, gathered, states_out, states, forward, applied, carried, carried_in,
-    carried_sum, back, back_in, behind_out, behind, near_entry, near_rhs,
+    carried_sum, offset, back_in, back_sum, behind_out, behind, own_coupling, own_carried,
     local_sem, exit_sem, part_send, part_recv, open_send, open_recv,
     comp_send, comp_recv, state_send, state_recv, fwd_send, fwd_recv,
-    car_send, car_recv, back_send, back_recv, beh_send, beh_recv, near_send, near_recv,
+    car_send, car_recv, back_send, back_recv, beh_send, beh_recv,
+    coup_send, coup_recv, sum_send, sum_recv,
 ):
     c = lax.axis_index("chain")
     k = lax.axis_index("col")
@@ -156,6 +157,16 @@
                 device_id_type=MESH,
             )
 
+    for d in range(1, chips):
+        @pl.when(is_hub & (q + d < chips))
+        def _():
+            for other in range(2):
+                for place in range(m):
+                    pl.semaphore_signal(
+                        barrier, 1, device_id={"chain": 2 * (q + d) + other, "col": place},
+                        device_id_type=MESH,
+                    )
+
     @pl.when(c == n - 1)
     def _():
         arriving[...] = jnp.zeros_like(arriving)
@@ -184,7 +195,7 @@
     for p in range(count - 1):
         part(p)
 
-    expected = 2 * m - 1 + jnp.where(has_beside, 1, 0) + jnp.where(is_hub, chips - 1, 0)
+    expected = 2 * q + 2 * m - 1 + jnp.where(has_beside, 1, 0) + jnp.where(is_hub, chips - 1, 0)
     pl.semaphore_wait(barrier, expected)
 
     send(c > 0, exits.at[0], arriving, exit_sem.at[0], exit_sem.at[1], {"chain": c - 1})
@@ -212,13 +223,11 @@
     sent(jnp.logical_not(is_hub), parts_in.at[0, pl.ds(0, 2), :, pl.ds(0, window)], part_send)
     sent(is_hub, parts_in.at[0, 0, :, pl.ds(0, window)], part_send)
 
-    is_end = (k == 0) | (k == m - 1)
-    for way, (at, to) in enumerate(((m - 2, m - 1), (1, 0))):
-        send(k == at, entry, near_entry, near_send.at[way, 0], near_recv.at[0], {"col": to})
-        send(k == at, rhs, near_rhs, near_send.at[way, 1], near_recv.at[1], {"col": to})
-        sent(k == at, entry, near_send.at[way, 0])
-        sent(k == at, rhs, near_send.at[way, 1])
-
+    added = pl.ds(0, half)
+    through = pl.ds(half, nx)
+    first_core = pl.ds(window, nx)
+    onward = pl.ds(0, window)
+    kept = pl.ds(half, 2 * nx)
     mine = pl.ds(pl.multiple_of(h * half, 8), window)
     source_rows = pl.ds(pl.multiple_of(h * window, 8), half)
 
@@ -263,77 +272,114 @@
         both = exact_dot(
             jnp.concatenate([prefix[last - 1], prefix_add[last - 1]], axis=0), coupling(last)
         )
-        comp[:nx] = both[:nx]
-        comp[nx:] = both[nx:] + source(last)
+        comp[through] = both[:nx]
+        comp[added] = both[nx:] + source(last)
+        comp[first_core] = prefix[count - 1]
 
         @pl.when(q == 0)
         def _():
-            comp[nx:] = exact_dot(states_out[0], comp[:nx]) + comp[nx:]
-
-    added = pl.ds(nx, half)
-    kept = pl.ds(0, nx)
+            comp[added] = exact_dot(states_out[0], comp[through]) + comp[added]
+
     for d in range(1, chips):
         to = lax.rem(q + d, chips)
         later = {"chain": 2 * to + 1}
         send(
-            is_hub & (q > 0) & (q + d < chips), comp, gathered.at[q], comp_send.at[to],
-            comp_recv.at[q], later,
-        )
-        sent(is_hub & (q > 0) & (q + d < chips), comp, comp_send.at[to])
+            is_hub & (q > 0) & (q + d < chips), comp.at[onward], gathered.at[q, onward],
+            comp_send.at[to], comp_recv.at[q], later,
+        )
+        sent(is_hub & (q > 0) & (q + d < chips), comp.at[onward], comp_send.at[to])
         send(
             is_hub & (q == 0), comp.at[added], gathered.at[q, added], comp_send.at[to],
             comp_recv.at[q], later,
         )
         sent(is_hub & (q == 0), comp.at[added], comp_send.at[to])
 
-    @pl.when(is_hub)
-    def _():
-        prepared(ahead, jnp.concatenate([prefix[j] for j in range(blocks - 1)], axis=1))
-
-        @pl.when(q > 0)
-        def _():
-            received(gathered.at[0, added], comp_recv.at[0])
-
-            def fold(s, state):
-                received(gathered.at[s], comp_recv.at[s])
-                return exact_dot(state, gathered[s, :nx]) + gathered[s, nx:]
-
-            states_out[0] = lax.fori_loop(1, q, fold, gathered[0, nx:])
-
-        spread_out = stacked(states_out[0], ahead[0], ahead[1], ahead[2], plain)
-        for j in range(1, blocks):
-            states_out[j] = spread_out[:, (j - 1) * nx:j * nx] + prefix_add[j - 1]
-
-    def spread(source_ref, target, sends, recvs, order):
+    def spread(condition, source_at, target_at, sends, recv_at, order):
         for p in order:
             for i in range(m):
                 to = jnp.where(h == 0, m - 1 - i, i)
                 send(
-                    is_hub, source_ref.at[p], target.at[p, h],
-                    sends.at[0], recvs.at[p], {"chain": 2 * q, "col": to},
+                    condition, source_at(0, p), target_at(p), sends.at[0], recv_at(p),
+                    {"chain": 2 * q, "col": to},
                 )
                 send(
-                    is_hub & (to != k), source_ref.at[count + p], target.at[p, h],
-                    sends.at[1], recvs.at[p], {"col": to},
+                    condition & (to != k), source_at(1, p), target_at(p), sends.at[1],
+                    recv_at(p), {"col": to},
                 )
 
+            @pl.when(condition)
+            def _():
+                target_at(p)[...] = source_at(1, p)[...]
+
+    def spread_sent(condition, sends, amount):
+        for owner, places in ((0, m), (1, m - 1)):
+            sent(
+                condition, carried_in.at[0, pl.ds(0, places), pl.ds(0, amount)],
+                sends.at[owner],
+            )
+
+    inner = range(1, count)
+    quarter = nx // 2
+    at_end = q == 0
+    shift = jnp.where(at_end, 1, 0)
+    spread(
+        is_hub,
+        lambda owner, i: sums.at[
+            owner * count + i + shift, pl.ds(pl.multiple_of(half + h * quarter, 8), quarter)
+        ],
+        lambda i: own_coupling.at[i, pl.ds(pl.multiple_of(h * quarter, 8), quarter)],
+        coup_send, lambda i: coup_recv.at[i], range(count - 1),
+    )
+    if count > 1:
+        for owner, places in ((0, m), (1, m - 1)):
+            sent(
+                is_hub,
+                parts_in.at[0, pl.ds(0, places), pl.ds(0, count - 1), pl.ds(0, quarter)],
+                coup_send.at[owner],
+            )
+
+    def couplings_arrive():
+        for i in range(count - 1):
             @pl.when(is_hub)
             def _():
-                target[p, h] = source_ref[count + p]
-
-        sent(is_hub, carried_in.at[0, pl.ds(0, m - 1)], sends.at[1])
-        sent(is_hub, carried_in.at[0], sends.at[0])
-
-    def arrive(target, p, recvs):
+                received(own_coupling.at[i, pl.ds(0, quarter)], coup_recv.at[i])
+
+            @pl.when(jnp.logical_not(is_hub))
+            def _():
+                received(own_coupling.at[i], coup_recv.at[i])
+
+    @pl.when(is_hub)
+    def _():
+        prepared(ahead, jnp.concatenate([prefix[j] for j in range(blocks - 1)], axis=1))
+
+        @pl.when(q > 0)
+        def _():
+            received(gathered.at[0, added], comp_recv.at[0])
+
+            def fold(s, state):
+                received(gathered.at[s, onward], comp_recv.at[s])
+                return exact_dot(state, gathered[s, through]) + gathered[s, added]
+
+            states_out[0] = lax.fori_loop(1, q, fold, gathered[0, added])
+
+        spread_out = stacked(states_out[0], ahead[0], ahead[1], ahead[2], plain)
+        for j in range(1, blocks):
+            states_out[j] = spread_out[:, (j - 1) * nx:j * nx] + prefix_add[j - 1]
+
+    def arrive(target, p, semaphore):
         @pl.when(is_hub)
         def _():
-            received(target.at[p, 0], recvs.at[p])
+            received(target.at[p, 0], semaphore)
 
         @pl.when(jnp.logical_not(is_hub))
         def _():
-            received(target.at[p], recvs.at[p])
-
-    spread(states_out, states, state_send, state_recv, range(count))
+            received(target.at[p], semaphore)
+
+    spread(
+        is_hub, lambda owner, p: states_out.at[owner * count + p],
+        lambda p: states.at[p, h], state_send, lambda p: state_recv.at[p], range(count),
+    )
+    spread_sent(is_hub, state_send, count)
 
     for d in range(1, chips):
         to = lax.rem(q - d + chips, chips)
@@ -348,38 +394,21 @@
     def leave(p, condition):
         for way, step in ((0, 1), (1, -1)):
             beyond = k + step
-            goes = (beyond >= 0) & (beyond < m) & jnp.logical_not(is_last(beyond))
+            goes = (beyond >= 0) & (beyond < m)
             for side, rows in enumerate(halves):
                 send(
                     goes & condition, forward.at[k, p, rows], forward.at[k, p, rows],
                     fwd_send.at[way], fwd_recv.at[k, p, side], {"col": beyond},
                 )
 
-    def is_last(position):
-        return (position == 0) | (position == m - 1)
-
     for place in range(m):
-        for way in range(2):
-            last = (m - 1, 0)[way]
-            if place == last:
-                continue
-            passed = (place + 1, m - place)[way]
-            beside_last = abs(place - last) == 1
-            if m > 3 and False:
-                for side in range(2):
-                    amount = passed - beside_last
-                    if side == 0:
-                        amount += (passed == 1) - (passed == m - 1)
-                    if amount > 0:
-                        sent(
-                            (k == place) & (core == side), forward.at[pl.ds(0, amount)],
-                            fwd_send.at[way],
-                        )
-            elif passed > beside_last:
-                sent(k == place, forward.at[pl.ds(0, passed - beside_last)], fwd_send.at[way])
+        if place < m - 1:
+            sent(k == place, forward.at[pl.ds(0, place + 1)], fwd_send.at[0])
+        if place > 0:
+            sent(k == place, forward.at[pl.ds(0, m - place)], fwd_send.at[1])
 
     for p in range(count):
-        arrive(states, p, state_recv)
+        arrive(states, p, state_recv.at[p])
         state = states[p].reshape(columns, nx)
         forward[k, p] = (rhs[p].astype(F32) - split_dot_t(state, entry[p])).astype(BF16)
         leave(p, core == 0)
@@ -391,25 +420,12 @@
         loads[4 + p].wait()
         applied[p] = dot_t(forward[k, p], block(k, p))
         leave(p, core == 1)
-    near = jnp.where(k == 0, 1, m - 2)
-
-    @pl.when(is_end)
-    def _():
-        received(near_entry, near_recv.at[0])
-        received(near_rhs, near_recv.at[1])
-        for p in range(count):
-            state = states[p].reshape(columns, nx)
-            near_block = near_rhs[p].astype(F32) - split_dot_t(state, near_entry[p])
-            applied[p] += dot_t(near_block.astype(BF16), block(near, p))
-
     def come(d, p):
         for side, rows in enumerate(halves):
             for way, step in ((0, 1), (1, -1)):
                 j = k - step * d
                 beyond = k + step
                 there = (j >= 0) & (j < m)
-                if d == 1:
-                    there &= jnp.logical_not(is_last(k))
 
                 @pl.when(there)
                 def _():
@@ -432,8 +448,6 @@
             for step in (1, -1):
                 j = k - step * d
                 there = (j >= 0) & (j < m)
-                if d == 1:
-                    there &= jnp.logical_not(is_last(k))
 
                 @pl.when(there)
                 def _():
@@ -452,32 +466,57 @@
     sent(jnp.logical_not(is_hub), carried_in.at[0, pl.ds(0, 2)], car_send)
     sent(is_hub, carried_in.at[0, 0], car_send)
 
+    @pl.when(jnp.logical_not(at_end))
+    def _():
+        couplings_arrive()
+        term = carried[count - 1]
+        for p in range(count - 2, -1, -1):
+            term = exact_dot_t(term, own_coupling[p]) + carried[p]
+        offset[...] = term
+
+    for t in range(chips - 1):
+        for side in far_first:
+            send(
+                t < q, offset.at[pl.ds(pl.multiple_of(side * half, 8), half)],
+                back_in.at[c, k], back_send, back_recv.at[c],
+                {"chain": 2 * t + 1, "col": mids[0] + side},
+            )
+        sent(q == t + 1, back_in.at[pl.ds(0, t + 1), pl.ds(0, 2)], back_send)
+
     own_rows = pl.ds(pl.multiple_of(h * half, 8), half)
+
+    others = [j for j in range(blocks - 1) if j != count - 1]
 
     @pl.when(is_hub)
     def _():
         suffix = [coupling(blocks - 1)]
         for j in range(blocks - 2, 0, -1):
             suffix.append(exact_dot(coupling(j), suffix[-1]))
+        suffix = suffix[::-1]
         same = lax.broadcasted_iota(jnp.int32, (nx, nx), 0) == lax.broadcasted_iota(
             jnp.int32, (nx, nx), 1
         )
-        reach[...] = jnp.concatenate(suffix[::-1] + [jnp.where(same, 1.0, 0.0)], axis=0)
+        reach[...] = jnp.concatenate(
+            [suffix[count - 1], jnp.where(same, 1.0, 0.0)] + [suffix[j] for j in others], axis=0
+        )
 
         def extend(s, carry):
-            at = pl.ds(pl.multiple_of((s - 1) * nx, 128), nx)
-            for i, term in enumerate(terms(reach[...])):
-                reach_terms[i, :, at] = term
             received(gathered.at[s, kept], comp_recv.at[s])
-            reach[...] = exact_dot(reach[...], gathered[s, :nx])
+
+            def keep(chain, value):
+                at = pl.ds(pl.multiple_of((chain - 2) * nx, 128), nx)
+                for i, term in enumerate(terms(value)):
+                    reach_terms[i, :, at] = term
+
+            keep(2 * s, reach[...])
+            keep(2 * s + 1, exact_dot(reach[...], gathered[s, first_core]))
+            reach[...] = exact_dot(reach[...], gathered[s, through])
             return carry
 
-        reach_terms[...] = jnp.zeros_like(reach_terms)
         lax.fori_loop(q + 1, chips, extend, 0)
 
     @pl.when(is_hub)
     def _():
-        offset = None
         for p in range(count):
             for owner in (1, 0):
                 j = owner * count + p
@@ -487,51 +526,90 @@
                     value = carried_in[owner, lax.rem(k + d, m), p]
                     total = value if total is None else total + value
                 carried_sum[j] = total
-                if j > 0:
-                    at = slice((j - 1) * nx, j * nx)
-                    total = stacked(
-                        total, ahead[0, :, at], ahead[1, :, at], ahead[2, :, at], dot_t
-                    )
-                offset = total if offset is None else offset + total
-        back[...] = offset
-
-    for d in range(1, chips):
-        to = lax.rem(q - d + chips, chips)
-        send(
-            is_hub & (q - d >= 0), back, back_in.at[q], back_send.at[d - 1],
-            back_recv.at[q], {"chain": 2 * to + 1},
-        )
-        sent(is_hub & (q - d >= 0), back, back_send.at[d - 1])
+
+    spread(
+        is_hub & at_end, lambda owner, p: carried_sum.at[owner * count + p],
+        lambda p: own_carried.at[p, h], sum_send, lambda p: sum_recv.at[p], inner,
+    )
+    if count > 1:
+        spread_sent(is_hub & at_end, sum_send, count - 1)
+
+    def bring(s, rows):
+        at = slice((2 * s - 2) * nx, 2 * s * nx)
+        return stacked(
+            jnp.concatenate([back_sum[2 * s - 2], back_sum[2 * s - 1]], axis=1),
+            reach_terms[0, rows, at], reach_terms[1, rows, at], reach_terms[2, rows, at],
+            dot_t,
+        )
+
+    later_chips = range(1, chips)
 
     @pl.when(is_hub)
     def _():
+        within = {blocks - 2: carried_sum[blocks - 1]}
+        for j in range(blocks - 3, -1, -1):
+            within[j] = exact_dot_t(within[j + 1], coupling(j + 1)) + carried_sum[j + 1]
+        for j in range(blocks - 1):
+            behind_out[j] = within[j]
+
         behind_out[blocks - 1] = jnp.zeros((half, nx), F32)
-        behind_out[blocks - 2] = carried_sum[blocks - 1]
-        for j in range(blocks - 3, -1, -1):
-            behind_out[j] = exact_dot_t(behind_out[j + 1], coupling(j + 1)) + carried_sum[j + 1]
-
-        for s in range(1, chips):
+        for s in later_chips:
             @pl.when(s > q)
             def _():
-                received(back_in.at[s], back_recv.at[s])
-
-            @pl.when(s <= q)
+                for chain in (2 * s, 2 * s + 1):
+                    received(back_in.at[chain], back_recv.at[chain])
+                    total = back_in[chain, 0]
+                    for d in range(1, m):
+                        total += back_in[chain, d]
+                    back_sum[chain - 2] = total
+                more = bring(s, slice(0, 2 * nx))
+                behind_out[count - 1] += more[:, :nx]
+                behind_out[blocks - 1] += more[:, nx:]
+
+    def outward(condition, order):
+        spread(
+            condition, lambda owner, p: behind_out.at[owner * count + p],
+            lambda p: behind.at[p, h], beh_send, lambda p: beh_recv.at[p], order,
+        )
+
+    outward(is_hub, [count - 1])
+    if count > 1:
+        for s in later_chips:
+            @pl.when(is_hub & (q > 0) & (s > q))
             def _():
-                back_in[s] = jnp.zeros((half, nx), F32)
-
-        more = stacked(
-            jnp.concatenate([back_in[s] for s in range(1, chips)], axis=1),
-            reach_terms[0], reach_terms[1], reach_terms[2], dot_t,
-        )
-        for j in range(blocks):
-            behind_out[j] += more[:, j * nx:(j + 1) * nx]
-
-    spread(behind_out, behind, beh_send, beh_recv, reversed(range(count)))
-
-    for p in reversed(range(count)):
-        arrive(behind, p, beh_recv)
-        state = behind[p].reshape(columns, nx)
+                more = bring(s, slice(2 * nx, blocks * nx))
+                for i, j in enumerate(others):
+                    behind_out[j] += more[:, i * nx:(i + 1) * nx]
+
+        outward(is_hub & (q > 0), reversed(range(count - 1)))
+    spread_sent(is_hub & at_end, beh_send, 1)
+    spread_sent(is_hub & (q > 0), beh_send, count)
+
+    @pl.when(at_end)
+    def _():
+        couplings_arrive()
+        for p in inner:
+            arrive(own_carried, p, sum_recv.at[p])
+
+    def finish(p, state):
         out_ref[p] = applied[p] - split_dot_t(state, following(p))
+
+    arrive(behind, count - 1, beh_recv.at[count - 1])
+    last_state = behind[count - 1].reshape(columns, nx)
+    finish(count - 1, last_state)
+
+    @pl.when(at_end)
+    def _():
+        state = last_state
+        for p in reversed(inner):
+            state = exact_dot_t(state, own_coupling[p - 1]) + own_carried[p].reshape(columns, nx)
+            finish(p - 1, state)
+
+    @pl.when(jnp.logical_not(at_end))
+    def _():
+        for p in reversed(range(count - 1)):
+            arrive(behind, p, beh_recv.at[p])
+            finish(p, behind[p].reshape(columns, nx))
 
     for condition, ref, semaphore in unsent:
         @pl.when(condition)
@@ -580,9 +658,9 @@
             vmem((rest, half, nx), F32),
             vmem((3, nx, rest * nx), BF16),
             vmem((blocks * nx, nx), F32),
-            vmem((3, blocks * nx, (chips - 1) * nx), BF16),
-            vmem((nx + half, nx), F32),
-            vmem((chips, nx + half, nx), F32),
+            vmem((3, blocks * nx, (n - 2) * nx), BF16),
+            vmem((2 * nx + half, nx), F32),
+            vmem((chips, 2 * nx + half, nx), F32),
             vmem((blocks, half, nx), F32),
             vmem((count, 2, half, nx), F32),
             vmem((m, count, columns, padded), BF16),
@@ -590,12 +668,13 @@
             vmem((count, columns, nx), F32),
             vmem((2, m, count, half, nx), F32),
             vmem((blocks, half, nx), F32),
-            vmem((half, nx), F32),
-            vmem((chips, half, nx), F32),
+            vmem((columns, nx), F32),
+            vmem((n, m, half, nx), F32),
+            vmem((n - 2, half, nx), F32),
             vmem((blocks, half, nx), F32),
             vmem((count, 2, half, nx), F32),
-            vmem(entry_factor.shape, BF16),
-            vmem((count, columns, padded), BF16),
+            vmem((count, nx, nx), F32),
+            vmem((count, 2, half, nx), F32),
             dma((4 + count,)),
             dma((2,)),
             dma(()), dma((blocks,)),
@@ -604,9 +683,10 @@
             dma((2,)), dma((count,)),
             dma((2,)), dma((m, count, 2)),
             dma(()), dma((blocks,)),
-            dma((chips - 1,)), dma((chips,)),
+            dma(()), dma((n,)),
             dma((2,)), dma((count,)),
-            dma((2, 2)), dma((2,)),
+            dma((2,)), dma((count,)),
+            dma((2,)), dma((count,)),
         ],
         compiler_params=pltpu.CompilerParams(
             collective_id=0, has_side_effects=True, vmem_limit_bytes=40 * 2**20

time: 44.8 us -> 43.5 us (0.971)
  Pallas kernels: 44 us -> 42.6 us
    pallas_call x1, Pallas kernels: 44 us -> 42.6 us  [shards(): pl.pallas_call(functools.partial(kernel, n, m), out_shape=pltpu.VMEM((cou...]
where the time goes in v4:
time: 43.5 us; the launch traced here: 43.4 us
  Pallas kernels  42.6 us (98%)
  local copies, waits for them, and re-layouts  0.73 us (2%)
    pallas_call x1, Pallas kernels, shards(): pl.pallas_call(functools.partial(kernel, n, m), out_shape=pltpu.VMEM((cou...  42.6 us

profile of v4, /device:TPU:0, one launch (start us, length us, event | category | flops | bytes accessed | tf_op | source)
XLA Modules:
  0.0 43.4 jit_solution(16720049029640274405)
XLA Ops:
  0.0 42.6 %shard_map.55 = f32[2,64,640]{2,1,0:T(8,128)S(1)} custom-call(bf16[2,64,640]{2,1,0:T(8,128)(2,1)} %rhs_hbm.1, bf16[2,640,2560]{2,1,0:T(8,128)(2,1)} %binv_hbm.1, bf16[2,640,128]{2,1,0:T(8,128)(2,1)} %entry_hbm.1, bf16[2,640,128]{2,1,0:T(8,128)(2,1)} %exit_hbm.1, bf16[64,640]{1,0:T(8,128)(2,1)} %prev_hbm.1), custom_call_target="tpu_custom_call" | custom-call | tf_op jit(solution)/shard_map/pallas_call | solution.py:640
  42.7 0.7 %copy.7 = f32[2,64,640]{2,1,0:T(8,128)} copy(f32[2,64,640]{2,1,0:T(8,128)S(1)} %shard_map.55) | data formatting | bytes 655360

commit v5 on v4

--- a/solution.py
+++ b/solution.py
@@ -72,11 +72,11 @@
     rhs, binv, entry, exits, prev, arriving,
     parts, parts_in, opening, opening_in, sums, prefix, prefix_add, ahead, reach, reach_terms,
     comp, gathered, states_out, states, forward, applied, carried, carried_in,
-    carried_sum, offset, back_in, back_sum, behind_out, behind, own_coupling, own_carried,
+    carried_sum, offset, back_in, back_sum, behind_out, behind, own_coupling, own_carried, through_exit, near_entry, near_rhs,
     local_sem, exit_sem, part_send, part_recv, open_send, open_recv,
     comp_send, comp_recv, state_send, state_recv, fwd_send, fwd_recv,
     car_send, car_recv, back_send, back_recv, beh_send, beh_recv,
-    coup_send, coup_recv, sum_send, sum_recv,
+    coup_send, coup_recv, sum_send, sum_recv, near_send, near_recv,
 ):
     c = lax.axis_index("chain")
     k = lax.axis_index("col")
@@ -222,6 +222,15 @@
             )
     sent(jnp.logical_not(is_hub), parts_in.at[0, pl.ds(0, 2), :, pl.ds(0, window)], part_send)
     sent(is_hub, parts_in.at[0, 0, :, pl.ds(0, window)], part_send)
+
+    early = core == 1
+    is_end = (k == 0) | (k == m - 1)
+    for way, (at, to) in enumerate(((m - 2, m - 1), (1, 0))):
+        give = (k == at) & early
+        send(give, entry, near_entry, near_send.at[way, 0], near_recv.at[0], {"col": to})
+        send(give, rhs, near_rhs, near_send.at[way, 1], near_recv.at[1], {"col": to})
+        sent(give, entry, near_send.at[way, 0])
+        sent(give, rhs, near_send.at[way, 1])
 
     added = pl.ds(0, half)
     through = pl.ds(half, nx)
@@ -389,29 +398,44 @@
         )
         sent(is_hub & (q - d >= 0), comp.at[kept], comp_send.at[to])
 
-    halves = [pl.ds(side * half, half) for side in range(2)]
-
-    def leave(p, condition):
+    cut = -(-width // 256) * 128
+    pieces = [(0, cut), (cut, width - cut)] if cut < width else [(0, width)]
+
+    def leave(p):
         for way, step in ((0, 1), (1, -1)):
             beyond = k + step
-            goes = (beyond >= 0) & (beyond < m)
-            for side, rows in enumerate(halves):
+            goes = (beyond >= 0) & (beyond < m) & jnp.logical_not(is_told(beyond))
+            for piece, (start, size) in enumerate(pieces):
+                part_ref = forward.at[k, p, :, pl.ds(start, size)]
                 send(
-                    goes & condition, forward.at[k, p, rows], forward.at[k, p, rows],
-                    fwd_send.at[way], fwd_recv.at[k, p, side], {"col": beyond},
+                    goes, part_ref, part_ref,
+                    fwd_send.at[way], fwd_recv.at[k, p, piece], {"col": beyond},
                 )
 
+    def is_told(position):
+        return ((position == 0) | (position == m - 1)) & early
+
     for place in range(m):
-        if place < m - 1:
-            sent(k == place, forward.at[pl.ds(0, place + 1)], fwd_send.at[0])
-        if place > 0:
-            sent(k == place, forward.at[pl.ds(0, m - place)], fwd_send.at[1])
+        for way, last in ((0, m - 1), (1, 0)):
+            if place == last:
+                continue
+            passed = (place + 1, m - place)[way]
+            held = 1 if abs(place - last) == 1 else 0
+            sent(
+                (k == place) & jnp.logical_not(early), forward.at[pl.ds(0, passed)],
+                fwd_send.at[way],
+            )
+            if passed > held:
+                sent(
+                    (k == place) & early, forward.at[pl.ds(0, passed - held)],
+                    fwd_send.at[way],
+                )
 
     for p in range(count):
         arrive(states, p, state_recv.at[p])
         state = states[p].reshape(columns, nx)
         forward[k, p] = (rhs[p].astype(F32) - split_dot_t(state, entry[p])).astype(BF16)
-        leave(p, core == 0)
+        leave(p)
 
     def block(j, p):
         return binv[p, :, pl.ds(pl.multiple_of(j * width, 128), width)]
@@ -419,39 +443,61 @@
     for p in range(count):
         loads[4 + p].wait()
         applied[p] = dot_t(forward[k, p], block(k, p))
-        leave(p, core == 1)
-    def come(d, p):
-        for side, rows in enumerate(halves):
-            for way, step in ((0, 1), (1, -1)):
-                j = k - step * d
-                beyond = k + step
-                there = (j >= 0) & (j < m)
-
-                @pl.when(there)
-                def _():
-                    received(forward.at[j, p, rows], fwd_recv.at[j, p, side])
-
-                if d + 1 < m:
-                    send(
-                        there & (beyond >= 0) & (beyond < m),
-                        forward.at[j, p, rows], forward.at[j, p, rows],
-                        fwd_send.at[way], fwd_recv.at[j, p, side], {"col": beyond},
-                    )
+    near = jnp.where(k == 0, 1, m - 2)
+
+    @pl.when(is_end & early)
+    def _():
+        received(near_entry, near_recv.at[0])
+        received(near_rhs, near_recv.at[1])
+        for p in range(count):
+            state = states[p].reshape(columns, nx)
+            near_block = near_rhs[p].astype(F32) - split_dot_t(state, near_entry[p])
+            applied[p] += dot_t(near_block.astype(BF16), block(near, p))
+
+    def come(d, p, piece):
+        start, size = pieces[piece]
+        for way, step in ((0, 1), (1, -1)):
+            j = k - step * d
+            beyond = k + step
+            there = (j >= 0) & (j < m)
+            if d == 1:
+                there &= jnp.logical_not(is_told(k))
+            part_ref = forward.at[j, p, :, pl.ds(start, size)]
+
+            @pl.when(there)
+            def _():
+                received(part_ref, fwd_recv.at[j, p, piece])
+
+            if d + 1 < m:
+                send(
+                    there & (beyond >= 0) & (beyond < m), part_ref, part_ref,
+                    fwd_send.at[way], fwd_recv.at[j, p, piece], {"col": beyond},
+                )
+
+    def multiply(d, p, start, size):
+        for step in (1, -1):
+            j = k - step * d
+            there = (j >= 0) & (j < m)
+            if d == 1:
+                there &= jnp.logical_not(is_told(k))
+
+            @pl.when(there)
+            def _():
+                at = pl.ds(pl.multiple_of(j * width + start, 128), size)
+                applied[p] += dot_t(forward[j, p, :, pl.ds(start, size)], binv[p, :, at])
 
     for d in range(1, m - 1):
         for p in range(count):
-            come(d, p)
+            for piece in range(len(pieces)):
+                come(d, p, piece)
     for d in range(1, m):
         for p in range(count):
-            if d + 1 == m:
-                come(d, p)
-            for step in (1, -1):
-                j = k - step * d
-                there = (j >= 0) & (j < m)
-
-                @pl.when(there)
-                def _():
-                    applied[p] += dot_t(forward[j, p], block(j, p))
+            if d + 1 < m:
+                multiply(d, p, 0, width)
+            else:
+                for piece, (start, size) in enumerate(pieces):
+                    come(d, p, piece)
+                    multiply(d, p, start, size)
             if d == m - 1:
                 carried[p] = jnp.dot(
                     applied[p].astype(BF16), entry[p], preferred_element_type=F32
@@ -590,23 +636,38 @@
         couplings_arrive()
         for p in inner:
             arrive(own_carried, p, sum_recv.at[p])
+        factor, remainder = None, None
+        for p in range(count - 2, -1, -1):
+            sum_here = own_carried[p + 1].reshape(columns, nx)
+            if factor is None:
+                factor, remainder = own_coupling[p], sum_here
+            else:
+                factor = exact_dot(own_coupling[p], factor)
+                remainder = exact_dot_t(remainder, own_coupling[p]) + sum_here
+            low = following(p)
+            c1, c2, c3 = terms(factor)
+            row = (plain(low, c3) + plain(low, c2)) + plain(low, c1)
+            for i, term in enumerate(terms(row)):
+                through_exit[p, i] = term
+            applied[p] = applied[p] - split_dot_t(remainder, low)
 
     def finish(p, state):
         out_ref[p] = applied[p] - split_dot_t(state, following(p))
 
     arrive(behind, count - 1, beh_recv.at[count - 1])
     last_state = behind[count - 1].reshape(columns, nx)
-    finish(count - 1, last_state)
 
     @pl.when(at_end)
     def _():
-        state = last_state
-        for p in reversed(inner):
-            state = exact_dot_t(state, own_coupling[p - 1]) + own_carried[p].reshape(columns, nx)
-            finish(p - 1, state)
+        for p in range(count - 1):
+            out_ref[p] = applied[p] - stacked(
+                last_state, through_exit[p, 0], through_exit[p, 1], through_exit[p, 2], dot_t
+            )
+        finish(count - 1, last_state)
 
     @pl.when(jnp.logical_not(at_end))
     def _():
+        finish(count - 1, last_state)
         for p in reversed(range(count - 1)):
             arrive(behind, p, beh_recv.at[p])
             finish(p, behind[p].reshape(columns, nx))
@@ -675,6 +736,9 @@
             vmem((count, 2, half, nx), F32),
             vmem((count, nx, nx), F32),
             vmem((count, 2, half, nx), F32),
+            vmem((count, 3, padded, nx), BF16),
+            vmem(entry_factor.shape, BF16),
+            vmem((count, columns, padded), BF16),
             dma((4 + count,)),
             dma((2,)),
             dma(()), dma((blocks,)),
@@ -687,6 +751,7 @@
             dma((2,)), dma((count,)),
             dma((2,)), dma((count,)),
             dma((2,)), dma((count,)),
+            dma((2, 2)), dma((2,)),
         ],
         compiler_params=pltpu.CompilerParams(
             collective_id=0, has_side_effects=True, vmem_limit_bytes=40 * 2**20

time: 43.5 us -> 42.6 us (0.979)
  Pallas kernels: 42.6 us -> 41.7 us
    pallas_call x1, Pallas kernels: 42.6 us -> 41.7 us  [shards(): pl.pallas_call(functools.partial(kernel, n, m), out_shape=pltpu.VMEM((cou...]
where the time goes in v5:
time: 42.6 us; the launch traced here: 42.4 us
  Pallas kernels  41.7 us (98%)
  local copies, waits for them, and re-layouts  0.73 us (2%)
    pallas_call x1, Pallas kernels, shards(): pl.pallas_call(functools.partial(kernel, n, m), out_shape=pltpu.VMEM((cou...  41.7 us

profile of v5, /device:TPU:0, one launch (start us, length us, event | category | flops | bytes accessed | tf_op | source)
XLA Modules:
  0.0 42.4 jit_solution(16922779384914516563)
XLA Ops:
  0.0 41.7 %shard_map.55 = f32[2,64,640]{2,1,0:T(8,128)S(1)} custom-call(bf16[2,64,640]{2,1,0:T(8,128)(2,1)} %rhs_hbm.1, bf16[2,640,2560]{2,1,0:T(8,128)(2,1)} %binv_hbm.1, bf16[2,640,128]{2,1,0:T(8,128)(2,1)} %entry_hbm.1, bf16[2,640,128]{2,1,0:T(8,128)(2,1)} %exit_hbm.1, bf16[64,640]{1,0:T(8,128)(2,1)} %prev_hbm.1), custom_call_target="tpu_custom_call" | custom-call | tf_op jit(solution)/shard_map/pallas_call | solution.py:701
  41.7 0.7 %copy.7 = f32[2,64,640]{2,1,0:T(8,128)} copy(f32[2,64,640]{2,1,0:T(8,128)S(1)} %shard_map.55) | data formatting | bytes 655360
